TPU v7x, 8 devices: a whole 2x2x1 slice. The times are simulated.
8 devices in a mesh: data: 1 (over z), ffn: 2 (over y), hid: 4 (over x, core).
Axes of the slice: x: 2, y: 2, z: 1, core: 2. Of those that a mesh axis runs over, the one named last changes fastest.
Arguments:
- residual: bfloat16 [64, 5120], P('data', 'hid')
- gain_mlp: float32 [5120], P('hid')
- gain_attn: float32 [5120], P('hid')
- w_gate: bfloat16 [5120, 13824], P('hid', 'ffn')
- w_up: bfloat16 [5120, 13824], P('hid', 'ffn')
- w_down: bfloat16 [13824, 5120], P('ffn', 'hid')
- w_qkv: bfloat16 [5120, 15360], P('hid', 'ffn')
Outputs:
- output 1: bfloat16 [64, 5120], P('data', 'hid')
- output 2: bfloat16 [64, 15360], P('data', 'ffn')
All inputs are finite; a program needn't handle non-finite values.
Results may differ from a plain program's by a relative error of at most 0.01852.
Values are sent between devices in bfloat16 or wider.
A program may use at most 1 GiB of HBM per device.

v0:
```python
import jax
import jax.numpy as jnp
from jax import lax
from jax.sharding import PartitionSpec as P

NORM_EPS = 1e-6


def solution(mesh):
    hid_ways = mesh.shape['hid']

    def shard_norm(resid_shard, gain_shard, d_model):
        resid32 = resid_shard.astype(jnp.float32)
        part_sq = jnp.sum(resid32 * resid32, axis=1, keepdims=True)
        full_sq = lax.psum(part_sq, 'hid')
        scale = lax.rsqrt(full_sq / d_model + NORM_EPS)
        return (resid32 * scale * gain_shard[None, :]).astype(jnp.bfloat16)

    def device_step(residual, gain_mlp, gain_attn, w_gate, w_up, w_down, w_qkv):
        d_model = residual.shape[1] * hid_ways
        normed = shard_norm(residual, gain_mlp, d_model)
        gate_part = jnp.dot(normed, w_gate, preferred_element_type=jnp.float32).astype(jnp.bfloat16)
        up_part = jnp.dot(normed, w_up, preferred_element_type=jnp.float32).astype(jnp.bfloat16)
        gate_sum, up_sum = lax.psum((gate_part, up_part), 'hid')
        hidden_act = (jax.nn.silu(gate_sum.astype(jnp.float32)) * up_sum.astype(jnp.float32)).astype(jnp.bfloat16)
        down_part = jnp.dot(hidden_act, w_down, preferred_element_type=jnp.float32).astype(jnp.bfloat16)
        down_sum = lax.psum(down_part, 'ffn')
        residual_out = (residual.astype(jnp.float32) + down_sum.astype(jnp.float32)).astype(jnp.bfloat16)
        normed_next = shard_norm(residual_out, gain_attn, d_model)
        qkv_part = jnp.dot(normed_next, w_qkv, preferred_element_type=jnp.float32).astype(jnp.bfloat16)
        qkv_out = lax.psum(qkv_part, 'hid')
        return residual_out, qkv_out

    return jax.shard_map(
        device_step, mesh=mesh,
        in_specs=(P('data', 'hid'), P('hid'), P('hid'), P('hid', 'ffn'), P('hid', 'ffn'),
                  P('ffn', 'hid'), P('hid', 'ffn')),
        out_specs=(P('data', 'hid'), P('data', 'ffn')),
        check_vma=False)
```

profile of v0, /device:TPU:0, one launch (start us, length us, event | category | flops | bytes accessed | tf_op | source)
XLA Modules:
  0.0 157.7 jit_solution(5696123217570960616)
XLA Ops:
  7.2 0.0 copy-start.1
  7.2 0.0 copy-start.3
  7.2 0.0 all-reduce.9.cloned.1.call-start
  7.2 1.1 fusion.10
  8.3 8.8 %psum.42 = f32[64,1]{0,1:T(1,128)S(1)} all-reduce(f32[64,1]{0,1:T(1,128)S(1)} %bitcast.11), channel_id=1, replica_groups=mesh['data'=1,'ffn'=2,'hid'=4] {'hid'}, use_global_device_ids=true, to_apply=%region_1.0 | all-reduce | flops 64 | bytes 512 | tf_op jit(solution)/shard_map/psum | solution.py:15
  17.1 0.0 copy-start
  17.1 10.5 %convolution_convert_fusion.1 = bf16[64,6912]{1,0:T(8,128)(2,1)} fusion(bf16[1280,6912]{1,0:T(8,128)(2,1)} %param.11, bf16[64,1280]{1,0:T(8,128)(2,1)} %param.7, f32[1280]{0:T(1024)} %param.8, f32[64]{0:T(128)S(1)} %rsqrt_bitcast_fusion.1), kind=kOutput, calls=%fused_computation.1 | convolution fusion | flops 1133232128 | bytes 18748672 | tf_op jit(solution)/shard_map/dot_general | solution.py:23
  27.5 0.0 copy-done.1
  27.5 0.0 copy-done.3
  27.5 1.0 copy-done
  28.5 4.1 %convolution_convert_fusion.2 = bf16[64,6912]{1,0:T(8,128)(2,1)} fusion(bf16[1280,6912]{1,0:T(8,128)(2,1)S(1)} %copy-done, bf16[64,1280]{1,0:T(8,128)(2,1)S(1)} %copy-done.1, f32[1280]{0:T(1024)S(1)} %copy-done.3, f32[64]{0:T(128)S(1)} %rsqrt_bitcast_fusion.1), kind=kOutput, calls=%fused_computation.2 | convolution fusion | flops 1133232128 | bytes 18748672 | tf_op jit(solution)/shard_map/dot_general | solution.py:22
  32.7 0.0 copy-start.4
  32.7 0.0 all-reduce.9.cloned.1.call-update
  32.7 0.0 all-reduce.5.cloned.1.call-start
  32.8 40.5 %all-reduce.9.cloned.1.call-done = (bf16[64,6912]{1,0:T(8,128)(2,1)}, bf16[64,6912]{1,0:T(8,128)(2,1)}) async-done(((bf16[64,6912]{1,0:T(8,128)(2,1)}, bf16[64,6912]{1,0:T(8,128)(2,1)}), (bf16[64,6912]{1,0:T(8,128)(2,1)}, bf16[64,6912]{1,0:T(8,128)(2,1)})) %all-reduce.9.cloned.1.call-update) | async-done | bytes 1769488 | tf_op jit(solution)/shard_map/psum | solution.py:24
  73.3 10.4 %convolution_convert_fusion.3 = bf16[64,1280]{1,0:T(8,128)(2,1)} fusion(bf16[6912,1280]{1,0:T(8,128)(2,1)} %param.12, bf16[64,6912]{1,0:T(8,128)(2,1)} %get-tuple-element.2, bf16[64,6912]{1,0:T(8,128)(2,1)} %get-tuple-element.3), kind=kOutput, calls=%fused_computation.3 | convolution fusion | flops 1136082944 | bytes 19628032 | tf_op jit(solution)/shard_map/dot_general | solution.py:26
  83.6 0.0 all-reduce.5.cloned.1.call-update
  83.7 0.0 all-reduce.7.cloned.1.call-start
  83.7 16.4 %all-reduce.5.cloned.1.call-done = bf16[64,1280]{1,0:T(8,128)(2,1)} async-done(((bf16[64,1280]{1,0:T(8,128)(2,1)}), bf16[64,1280]{1,0:T(8,128)(2,1)}) %all-reduce.5.cloned.1.call-update) | async-done | bytes 163856 | tf_op jit(solution)/shard_map/psum | solution.py:27
  100.1 1.1 fusion.7
  101.2 0.0 copy-start.2
  101.2 6.1 %psum.46 = f32[64,1]{0,1:T(1,128)S(1)} all-reduce(f32[64,1]{0,1:T(1,128)S(1)} %bitcast.10), channel_id=1, replica_groups=mesh['data'=1,'ffn'=2,'hid'=4] {'hid'}, use_global_device_ids=true, to_apply=%region_6.7 | all-reduce | flops 64 | bytes 512 | tf_op jit(solution)/shard_map/psum | solution.py:15
  107.3 0.0 copy-done.4
  107.3 11.2 %convolution_convert_fusion = bf16[64,7680]{1,0:T(8,128)(2,1)} fusion(bf16[1280,7680]{1,0:T(8,128)(2,1)} %param.13, bf16[64,1280]{1,0:T(8,128)(2,1)S(1)} %get-tuple-element.6, f32[1280]{0:T(1024)S(1)} %copy-done.4, f32[64]{0:T(128)S(1)} %rsqrt_bitcast_fusion), kind=kOutput, calls=%fused_computation | convolution fusion | flops 1259110400 | bytes 20813056 | tf_op jit(solution)/shard_map/dot_general | solution.py:30
  118.5 0.0 all-reduce.7.cloned.1.call-update
  118.5 30.5 %all-reduce.7.cloned.1.call-done = bf16[64,7680]{1,0:T(8,128)(2,1)} async-done(((bf16[64,7680]{1,0:T(8,128)(2,1)}), bf16[64,7680]{1,0:T(8,128)(2,1)}) %all-reduce.7.cloned.1.call-update) | async-done | bytes 983056 | tf_op jit(solution)/shard_map/psum | solution.py:31
  149.0 2.2 %copy.13 = bf16[64,7680]{1,0:T(8,128)(2,1)} copy(bf16[64,7680]{1,0:T(8,128)(2,1)} %all-reduce.7.cloned.1.call-done) | data formatting | bytes 1966080
  151.2 0.0 copy-done.2
  (2 shorter events, 0.0 us)
Async XLA Ops:
  7.2 20.4 %copy-start.1 = (bf16[64,1280]{1,0:T(8,128)(2,1)S(1)}, bf16[64,1280]{1,0:T(8,128)(2,1)}, u32[]{:S(2)}) copy-start(bf16[64,1280]{1,0:T(8,128)(2,1)} %param.7) | copy-start | bytes 491524
  7.2 20.4 %copy-start.3 = (f32[1280]{0:T(1024)S(1)}, f32[1280]{0:T(1024)}, u32[]{:S(2)}) copy-start(f32[1280]{0:T(1024)} %param.8) | copy-start | bytes 15364
  7.2 66.1 %all-reduce.9.cloned.1.call-start = ((), (), s32[]{:S(2)}) async-start(), calls=%async_computation.2 | async-start | bytes 3538944 | tf_op jit(solution)/shard_map/psum | solution.py:24
  17.1 11.5 %copy-start = (bf16[1280,6912]{1,0:T(8,128)(2,1)S(1)}, bf16[1280,6912]{1,0:T(8,128)(2,1)}, u32[]{:S(2)}) copy-start(bf16[1280,6912]{1,0:T(8,128)(2,1)} %param.10) | copy-start | bytes 53084164
  32.7 74.6 %copy-start.4 = (f32[1280]{0:T(1024)S(1)}, f32[1280]{0:T(1024)}, u32[]{:S(2)}) copy-start(f32[1280]{0:T(1024)} %param.9) | copy-start | bytes 15364
  32.7 67.4 %all-reduce.5.cloned.1.call-start = ((), (), s32[]{:S(2)}) async-start(), calls=%async_computation | async-start | bytes 327680 | tf_op jit(solution)/shard_map/psum | solution.py:27
  83.7 65.3 %all-reduce.7.cloned.1.call-start = ((), (), s32[]{:S(2)}) async-start(), calls=%async_computation.1 | async-start | bytes 1966080 | tf_op jit(solution)/shard_map/psum | solution.py:31
  101.2 50.0 %copy-start.2 = (bf16[64,1280]{1,0:T(8,128)(2,1)}, bf16[64,1280]{1,0:T(8,128)(2,1)S(1)}, u32[]{:S(2)}) copy-start(bf16[64,1280]{1,0:T(8,128)(2,1)S(1)} %get-tuple-element.6) | copy-start | bytes 491524
Sparse Core Ops, SparseCore 0:
  32.8 40.3 all-reduce.8
  83.8 16.2 all-reduce.4
  118.6 30.2 all-reduce.6
where the time goes:
time: 158 us
  waiting for transfers between devices  87.4 us (55%)
  matrix products  36.1 us (23%)
  blocking collectives  14.8 us (9%)
  between operations  13.8 us (9%)
  local copies, waits for them, and re-layouts  3.23 us (2%)
  other arithmetic  2.17 us (1%)
    psum x1, waiting for transfers between devices, device_step(): gate_sum, up_sum = lax.psum((gate_part, up_part), 'hid')  40.5 us
    psum x1, waiting for transfers between devices, device_step(): qkv_out = lax.psum(qkv_part, 'hid')  30.5 us
    psum x1, waiting for transfers between devices, device_step(): down_sum = lax.psum(down_part, 'ffn')  16.4 us
    psum x2, blocking collectives, shard_norm(): full_sq = lax.psum(part_sq, 'hid')  14.8 us
    dot_general x1, matrix products, device_step(): jnp.dot(normed_next, w_qkv, preferred_element_type=jnp.float32)  11.2 us
    dot_general x1, matrix products, device_step(): jnp.dot(normed, w_up, preferred_element_type=jnp.float32)  10.5 us
    dot_general x1, matrix products, device_step(): jnp.dot(hidden_act, w_down, preferred_element_type=jnp.float32)  10.4 us
    dot_general x1, matrix products, device_step(): jnp.dot(normed, w_gate, preferred_element_type=jnp.float32)  4.14 us
  transfers between devices with their start and end apart: 3, of which 3 were waited for; matrix products, arithmetic and copies ran while one was open for 0% of the time, Pallas kernels for 0%

commit v1 on v0

v1 whole, which is shorter than its diff:
```python
import functools

import jax
import jax.numpy as jnp
from jax import lax
from jax.experimental import pallas as pl
from jax.experimental.pallas import tpu as pltpu
from jax.sharding import PartitionSpec as P

NORM_EPS = 1e-6
MESH = pl.DeviceIdType.MESH
F32 = jnp.float32
BF16 = jnp.bfloat16

GC = 768
SLOTS = 5
QC = 768
DN = 256


def dot(a, b):
    return jnp.dot(a, b, preferred_element_type=F32)


def kernel(d_model, x_hbm, g1_hbm, g2_hbm, wg_hbm, wu_hbm, wd_hbm, wq_hbm, x2_hbm, q_hbm,
           xb, g1, g2, nb, wgu, wd, wq, p_buf, p_rcv, s_buf, s_rcv, a_buf, acc,
           dn_snd, dn_rcv, st_snd, st_all, qp, qp_rcv, qs, qs_rcv, qo,
           in_sem, wgu_sem, wd_sem, wq_sem, out_sem,
           p_ss, p_rs, s_ss, s_rs, ax_ss, ax_rs, ad_ss, ad_rs,
           dn_ss, dn_rs, st_ss, st_rs, qp_ss, qp_rs, qs_ss, qs_rs, qo_ss, qo_rs):
    rows, width = xb.shape
    half = rows // 2
    n_g = wg_hbm.shape[1] // GC
    n_q = wq_hbm.shape[1] // QC
    n_d = width // DN
    hc = GC // 2

    me = lax.axis_index('hid')
    y = lax.axis_index('ffn')
    z = lax.axis_index('data')
    chip = me // 2
    core = me % 2
    own = (core + chip) % 2
    other = 1 - own
    sib = (z, y, chip * 2 + (1 - core))
    partner = (z, y, (1 - chip) * 2 + (1 - core))
    ypeer = (z, 1 - y, me)

    def rcopy(src, dst, ss, rs, dev):
        return pltpu.make_async_remote_copy(src_ref=src, dst_ref=dst, send_sem=ss, recv_sem=rs,
                                            device_id=dev, device_id_type=MESH)

    def gu_copies(j):
        cols = pl.ds(j * GC, GC)
        return [pltpu.make_async_copy(w.at[:, cols], wgu.at[j % SLOTS, i], wgu_sem.at[j, i])
                for i, w in enumerate((wg_hbm, wu_hbm))]

    def wd_copy(j):
        r = pl.ds(j * GC, GC)
        return pltpu.make_async_copy(wd_hbm.at[r, :], wd.at[r, :], wd_sem.at[j])

    def wq_copy(j):
        return pltpu.make_async_copy(wq_hbm.at[:, pl.ds(j * QC, QC)], wq.at[j], wq_sem.at[j])

    later = [wd_copy(j) for j in range(n_g)] + [wq_copy(j) for j in range(n_q)]

    ins = [pltpu.make_async_copy(s, d, in_sem.at[i])
           for i, (s, d) in enumerate(((x_hbm, xb), (g1_hbm, g1), (g2_hbm, g2)))]
    for c in ins:
        c.start()
    for j in range(SLOTS):
        for c in gu_copies(j):
            c.start()

    barrier = pltpu.get_barrier_semaphore()
    hid_peers = [(z, y, (me + k) % 4) for k in (1, 2, 3)]
    for dev in hid_peers + [ypeer]:
        pl.semaphore_signal(barrier, inc=1, device_id=dev, device_id_type=MESH)

    def stat_send(t, sq):
        cols = jnp.sum(sq.T, axis=0, keepdims=True)
        st_snd[t] = jnp.broadcast_to(jnp.concatenate([cols, cols], axis=1), (8, 128))
        cps = [rcopy(st_snd.at[t], st_all.at[t, me], st_ss.at[t, k], st_rs.at[t, me], dev)
               for k, dev in enumerate(hid_peers)]
        for c in cps:
            c.start()
        st_all[t, me] = st_snd[t]
        return cps

    def stat_recv(t, cps):
        for k in (1, 2, 3):
            src = (me + k) % 4
            rcopy(st_snd.at[t], st_all.at[t, src], st_ss.at[t, k - 1], st_rs.at[t, src],
                  hid_peers[k - 1]).wait_recv()
        for c in cps:
            c.wait_send()
        total = (st_all[t, 0] + st_all[t, 1]) + (st_all[t, 2] + st_all[t, 3])
        scale = lax.rsqrt(total / d_model + NORM_EPS)
        return scale.T[:rows, 0:1]

    def lane_sq(v):
        out = None
        for k in range(v.shape[1] // 128):
            t = v[:, k * 128:(k + 1) * 128]
            out = t * t if out is None else out + t * t
        return out

    for c in ins:
        c.wait()
    sq1 = lane_sq(xb[...].astype(F32))
    pl.semaphore_wait(barrier, 4)
    cps = stat_send(0, sq1)
    scale1 = stat_recv(0, cps)
    nb[...] = (xb[...].astype(F32) * scale1 * g1[...]).astype(BF16)

    sends = []

    def compute(j):
        for i, c in enumerate(gu_copies(j)):
            c.wait()
            part = dot(nb[...], wgu[j % SLOTS, i]).astype(BF16)
            p_buf[j, 0, i] = part[:half]
            p_buf[j, 1, i] = part[half:]
        c = rcopy(p_buf.at[j, other], p_rcv.at[j], p_ss.at[j], p_rs.at[j], sib)
        c.start()
        sends.append(c)
        if j + SLOTS < n_g:
            for c in gu_copies(j + SLOTS):
                c.start()
        else:
            for _ in range(4):
                if later:
                    later.pop(0).start()

    def pair_sum(j):
        rcopy(p_buf.at[j, other], p_rcv.at[j], p_ss.at[j], p_rs.at[j], sib).wait_recv()
        for i in range(2):
            s = (p_buf[j, own, i].astype(F32) + p_rcv[j, i].astype(F32)).astype(BF16)
            s_buf[j, 0, i] = s[:, :hc]
            s_buf[j, 1, i] = s[:, hc:]
        c = rcopy(s_buf.at[j, 1 - chip], s_rcv.at[j], s_ss.at[j], s_rs.at[j], partner)
        c.start()
        sends.append(c)

    def a_piece(j, rh, ch):
        r = pl.ds(pl.multiple_of(rh * half, half), half)
        k = pl.ds(pl.multiple_of(j * GC + ch * hc, 128), hc)
        return a_buf.at[r, k]

    def act(j):
        rcopy(s_buf.at[j, 1 - chip], s_rcv.at[j], s_ss.at[j], s_rs.at[j], partner).wait_recv()
        g, u = [(s_buf[j, chip, i].astype(F32) + s_rcv[j, i].astype(F32)).astype(BF16).astype(F32)
                for i in range(2)]
        piece = a_piece(j, own, chip)
        piece[...] = (jax.nn.silu(g) * u).astype(BF16)
        c = rcopy(piece, piece, ax_ss.at[j], ax_rs.at[j], partner)
        c.start()
        sends.append(c)
        c = rcopy(piece, piece, ad_ss.at[j, 0], ad_rs.at[j, 0], sib)
        c.start()
        sends.append(c)

    def relay(j):
        piece = a_piece(j, own, 1 - chip)
        rcopy(piece, piece, ax_ss.at[j], ax_rs.at[j], partner).wait_recv()
        c = rcopy(piece, piece, ad_ss.at[j, 1], ad_rs.at[j, 1], sib)
        c.start()
        sends.append(c)

    def gathered(j):
        for t, ch in ((0, chip), (1, 1 - chip)):
            piece = a_piece(j, other, ch)
            rcopy(piece, piece, ad_ss.at[j, t], ad_rs.at[j, t], sib).wait_recv()

    def down(j0, j1, first):
        k = pl.ds(j0 * GC, (j1 - j0) * GC)
        for j in range(j0, j1):
            gathered(j)
            wd_copy(j).wait()
        part = dot(a_buf[:, k], wd[k, :])
        acc[...] = part if first else acc[...] + part

    for t in range(n_g + 7):
        if t < n_g:
            compute(t)
        if 0 <= t - 1 < n_g:
            pair_sum(t - 1)
        if 0 <= t - 3 < n_g:
            act(t - 3)
        if 0 <= t - 5 < n_g:
            relay(t - 5)
        if t == 9:
            down(0, 3, True)
        if t == 12:
            down(3, 6, False)
    while later:
        later.pop(0).start()

    k = pl.ds(6 * GC, (n_g - 6) * GC)
    for j in range(6, n_g):
        gathered(j)
        wd_copy(j).wait()
    dn_cps = []
    for n in range(n_d):
        cols = pl.ds(n * DN, DN)
        dn_snd[n] = (acc[:, cols] + dot(a_buf[:, k], wd[k, cols])).astype(BF16)
        c = rcopy(dn_snd.at[n], dn_rcv.at[n], dn_ss.at[n], dn_rs.at[n], ypeer)
        c.start()
        dn_cps.append(c)
    sq2 = None
    for n in range(n_d):
        cols = pl.ds(n * DN, DN)
        dn_cps[n].wait_recv()
        dn = (dn_snd[n].astype(F32) + dn_rcv[n].astype(F32)).astype(BF16)
        x2 = (xb[:, cols].astype(F32) + dn.astype(F32)).astype(BF16)
        nb[:, cols] = x2
        s = lane_sq(x2.astype(F32))
        sq2 = s if sq2 is None else sq2 + s
    cps = stat_send(1, sq2)
    x2_out = pltpu.make_async_copy(nb, x2_hbm, out_sem.at[0])
    x2_out.start()
    scale2 = stat_recv(1, cps)
    n2 = (nb[...].astype(F32) * scale2 * g2[...]).astype(BF16)
    xb[...] = n2

    outs = []

    def q_piece(j):
        return q_hbm.at[pl.ds(pl.multiple_of(own * half, half), half), pl.ds(j * QC, QC)]

    def q_other(j):
        return q_hbm.at[pl.ds(pl.multiple_of(other * half, half), half), pl.ds(j * QC, QC)]

    def q_compute(j):
        wq_copy(j).wait()
        part = dot(xb[...], wq[j]).astype(BF16)
        qp[j, 0] = part[:half]
        qp[j, 1] = part[half:]
        c = rcopy(qp.at[j, other], qp_rcv.at[j], qp_ss.at[j], qp_rs.at[j], sib)
        c.start()
        sends.append(c)

    def q_sum(j):
        rcopy(qp.at[j, other], qp_rcv.at[j], qp_ss.at[j], qp_rs.at[j], sib).wait_recv()
        qs[j] = (qp[j, own].astype(F32) + qp_rcv[j].astype(F32)).astype(BF16)
        c = rcopy(qs.at[j], qs_rcv.at[j], qs_ss.at[j], qs_rs.at[j], partner)
        c.start()
        sends.append(c)

    def q_final(j):
        rcopy(qs.at[j], qs_rcv.at[j], qs_ss.at[j], qs_rs.at[j], partner).wait_recv()
        qo[j] = (qs[j].astype(F32) + qs_rcv[j].astype(F32)).astype(BF16)
        c = pltpu.make_async_copy(qo.at[j], q_piece(j), out_sem.at[1 + j])
        c.start()
        outs.append(c)
        c = rcopy(qo.at[j], q_piece(j), qo_ss.at[j], qo_rs.at[j], sib)
        c.start()
        sends.append(c)

    for t in range(n_q + 3):
        if t < n_q:
            q_compute(t)
        if 0 <= t - 1 < n_q:
            q_sum(t - 1)
        if 0 <= t - 3 < n_q:
            q_final(t - 3)

    for j in range(n_q):
        rcopy(qo.at[j], q_other(j), qo_ss.at[j], qo_rs.at[j], sib).wait_recv()
    for c in outs:
        c.wait()
    x2_out.wait()
    for c in sends:
        c.wait_send()
    for c in dn_cps:
        c.wait_send()


def solution(mesh):
    hid_ways = mesh.shape['hid']

    def device_step(residual, gain_mlp, gain_attn, w_gate, w_up, w_down, w_qkv):
        rows, width = residual.shape
        ff = w_gate.shape[1]
        qn = w_qkv.shape[1]
        half = rows // 2
        n_g, n_q, n_d = ff // GC, qn // QC, width // DN
        dma = pltpu.SemaphoreType.DMA
        any_spec = pl.BlockSpec(memory_space=pltpu.HBM)
        return pl.pallas_call(
            functools.partial(kernel, width * hid_ways),
            out_shape=(jax.ShapeDtypeStruct((rows, width), BF16),
                       jax.ShapeDtypeStruct((rows, qn), BF16)),
            in_specs=[any_spec] * 7,
            out_specs=(any_spec, any_spec),
            scratch_shapes=[
                pltpu.VMEM((rows, width), BF16),
                pltpu.VMEM((1, width), F32),
                pltpu.VMEM((1, width), F32),
                pltpu.VMEM((rows, width), BF16),
                pltpu.VMEM((SLOTS, 2, width, GC), BF16),
                pltpu.VMEM((ff, width), BF16),
                pltpu.VMEM((n_q, width, QC), BF16),
                pltpu.VMEM((n_g, 2, 2, half, GC), BF16),
                pltpu.VMEM((n_g, 2, half, GC), BF16),
                pltpu.VMEM((n_g, 2, 2, half, GC // 2), BF16),
                pltpu.VMEM((n_g, 2, half, GC // 2), BF16),
                pltpu.VMEM((rows, ff), BF16),
                pltpu.VMEM((rows, width), F32),
                pltpu.VMEM((n_d, rows, DN), BF16),
                pltpu.VMEM((n_d, rows, DN), BF16),
                pltpu.VMEM((2, 8, 128), F32),
                pltpu.VMEM((2, 4, 8, 128), F32),
                pltpu.VMEM((n_q, 2, half, QC), BF16),
                pltpu.VMEM((n_q, half, QC), BF16),
                pltpu.VMEM((n_q, half, QC), BF16),
                pltpu.VMEM((n_q, half, QC), BF16),
                pltpu.VMEM((n_q, half, QC), BF16),
                dma((3,)), dma((n_g, 2)), dma((n_g,)), dma((n_q,)), dma((1 + n_q,)),
                dma((n_g,)), dma((n_g,)), dma((n_g,)), dma((n_g,)),
                dma((n_g,)), dma((n_g,)), dma((n_g, 2)), dma((n_g, 2)),
                dma((n_d,)), dma((n_d,)), dma((2, 3)), dma((2, 4)),
                dma((n_q,)), dma((n_q,)), dma((n_q,)), dma((n_q,)), dma((n_q,)), dma((n_q,)),
            ],
            compiler_params=pltpu.CompilerParams(
                collective_id=0, has_side_effects=True, vmem_limit_bytes=67043328),
        )(residual, gain_mlp[None, :], gain_attn[None, :], w_gate, w_up, w_down, w_qkv)

    return jax.shard_map(
        device_step, mesh=mesh,
        in_specs=(P('data', 'hid'), P('hid'), P('hid'), P('hid', 'ffn'), P('hid', 'ffn'),
                  P('ffn', 'hid'), P('hid', 'ffn')),
        out_specs=(P('data', 'hid'), P('data', 'ffn')),
        check_vma=False)
```

time: 158 us -> 67.1 us (0.42)
  waiting for transfers between devices: 87.4 us -> 0 us
  Pallas kernels: 0 us -> 59.8 us
  matrix products: 36.1 us -> 0 us
  blocking collectives: 14.8 us -> 0 us
  between operations: 13.8 us -> 0.64 us
  local copies, waits for them, and re-layouts: 3.23 us -> 6.39 us
  other arithmetic: 2.17 us -> 0 us
    psum x3 -> x0, waiting for transfers between devices: 87.3 us -> none  [the longest x1 40.5 us: device_step(): gate_sum, up_sum = lax.psum((gate_part, up_part), 'hid')]
    pallas_call x0 -> x1, Pallas kernels: none -> 59.8 us  [device_step(): pl.pallas_call(functools.partial(kernel, width * hid_ways), out_shape=(ja...]
    dot_general x4 -> x0, matrix products: 36.1 us -> none  [the longest x1 11.2 us: device_step(): jnp.dot(normed_next, w_qkv, preferred_element_type=jnp.float32)]
    psum x2 -> x0, blocking collectives: 14.8 us -> none  [shard_norm(): full_sq = lax.psum(part_sq, 'hid')]
    broadcast_in_dim x0 -> x2, local copies, waits for them, and re-layouts: none -> 2.59 us  [the longest x1 1.29 us: device_step(): gain_mlp[None, :]]
    reduce_sum x2 -> x0, other arithmetic: 2.15 us -> none  [shard_norm(): part_sq = jnp.sum(resid32 * resid32, axis=1, keepdims=True)]
    unnamed x11 -> x2, local copies, waits for them, and re-layouts: 3.23 us -> 3.8 us
  transfers between devices with their start and end apart: 3 -> 0, of which waited for: 3 -> 0; matrix products, arithmetic and copies ran while one was open for 0% -> 0% of each run, Pallas kernels for 0% -> 0%
where the time goes in v1:
time: 67.1 us; the launch traced here: 66.9 us
  Pallas kernels  59.8 us (89%)
  local copies, waits for them, and re-layouts  6.39 us (10%)
    pallas_call x1, Pallas kernels, device_step(): pl.pallas_call(functools.partial(kernel, width * hid_ways), out_shape=(ja...  59.8 us
    unnamed x2, local copies, waits for them, and re-layouts  3.8 us

profile of v1, /device:TPU:0, one launch (start us, length us, event | category | flops | bytes accessed | tf_op | source)
XLA Modules:
  0.0 66.9 jit_solution(11968168417969439557)
XLA Ops:
  0.6 1.3 %broadcast_in_dim.6.g1_hbm = f32[1,1280]{1,0:T(1,128)} reshape(f32[1280]{0:T(1024)} %param.8) | data formatting | bytes 10240 | tf_op jit(solution)/shard_map/broadcast_in_dim | solution.py:327
  1.9 1.3 %broadcast_in_dim.7.g2_hbm = f32[1,1280]{1,0:T(1,128)} reshape(f32[1280]{0:T(1024)} %param.9) | data formatting | bytes 10240 | tf_op jit(solution)/shard_map/broadcast_in_dim | solution.py:327
  3.2 59.8 %shard_map.86 = (bf16[64,1280]{1,0:T(8,128)(2,1)}, bf16[64,7680]{1,0:T(8,128)(2,1)}) custom-call(bf16[64,1280]{1,0:T(8,128)(2,1)} %x_hbm.1, f32[1,1280]{1,0:T(1,128)} %broadcast_in_dim.6.g1_hbm, f32[1,1280]{1,0:T(1,128)} %broadcast_in_dim.7.g2_hbm, bf16[1280,6912]{1,0:T(8,128)(2,1)} %wg_hbm.1, bf16[1280,6912]{1,0:T(8,128)(2,1)} %wu_hbm.1, ...), custom_call_target="tpu_custom_call" | custom-call | tf_op jit(solution)/shard_map/pallas_call | solution.py:290
  63.1 1.6 %copy.11 = bf16[64,1280]{1,0:T(8,128)(2,1)} copy(bf16[64,1280]{1,0:T(8,128)(2,1)} %get-tuple-element.4) | data formatting | bytes 327680
  64.6 2.2 %copy.12 = bf16[64,7680]{1,0:T(8,128)(2,1)} copy(bf16[64,7680]{1,0:T(8,128)(2,1)} %get-tuple-element.5) | data formatting | bytes 1966080

commit v2 on v1

--- a/solution.py
+++ b/solution.py
@@ -22,10 +22,10 @@
     return jnp.dot(a, b, preferred_element_type=F32)
 
 
-def kernel(d_model, x_hbm, g1_hbm, g2_hbm, wg_hbm, wu_hbm, wd_hbm, wq_hbm, x2_hbm, q_hbm,
+def kernel(d_model, x_hbm, g1_hbm, g2_hbm, wg_hbm, wu_hbm, wd_hbm, wq_hbm, x2_out, q_out,
            xb, g1, g2, nb, wgu, wd, wq, p_buf, p_rcv, s_buf, s_rcv, a_buf, acc,
-           dn_snd, dn_rcv, st_snd, st_all, qp, qp_rcv, qs, qs_rcv, qo,
-           in_sem, wgu_sem, wd_sem, wq_sem, out_sem,
+           dn_snd, dn_rcv, st_snd, st_all,
+           in_sem, wgu_sem, wd_sem, wq_sem,
            p_ss, p_rs, s_ss, s_rs, ax_ss, ax_rs, ad_ss, ad_rs,
            dn_ss, dn_rs, st_ss, st_rs, qp_ss, qp_rs, qs_ss, qs_rs, qo_ss, qo_rs):
     rows, width = xb.shape
@@ -70,7 +70,7 @@
         c.start()
     for j in range(SLOTS):
         for c in gu_copies(j):
-            c.start()
+            c.start(priority=1)
 
     barrier = pltpu.get_barrier_semaphore()
     hid_peers = [(z, y, (me + k) % 4) for k in (1, 2, 3)]
@@ -111,7 +111,7 @@
     pl.semaphore_wait(barrier, 4)
     cps = stat_send(0, sq1)
     scale1 = stat_recv(0, cps)
-    nb[...] = (xb[...].astype(F32) * scale1 * g1[...]).astype(BF16)
+    nb[...] = (xb[...].astype(F32) * scale1 * g1[...][None, :]).astype(BF16)
 
     sends = []
 
@@ -126,11 +126,11 @@
         sends.append(c)
         if j + SLOTS < n_g:
             for c in gu_copies(j + SLOTS):
-                c.start()
+                c.start(priority=1)
         else:
             for _ in range(4):
                 if later:
-                    later.pop(0).start()
+                    later.pop(0).start(priority=1)
 
     def pair_sum(j):
         rcopy(p_buf.at[j, other], p_rcv.at[j], p_ss.at[j], p_rs.at[j], sib).wait_recv()
@@ -194,7 +194,7 @@
         if t == 12:
             down(3, 6, False)
     while later:
-        later.pop(0).start()
+        later.pop(0).start(priority=1)
 
     k = pl.ds(6 * GC, (n_g - 6) * GC)
     for j in range(6, n_g):
@@ -213,47 +213,51 @@
         dn_cps[n].wait_recv()
         dn = (dn_snd[n].astype(F32) + dn_rcv[n].astype(F32)).astype(BF16)
         x2 = (xb[:, cols].astype(F32) + dn.astype(F32)).astype(BF16)
-        nb[:, cols] = x2
+        x2_out[:, cols] = x2
         s = lane_sq(x2.astype(F32))
         sq2 = s if sq2 is None else sq2 + s
     cps = stat_send(1, sq2)
-    x2_out = pltpu.make_async_copy(nb, x2_hbm, out_sem.at[0])
-    x2_out.start()
     scale2 = stat_recv(1, cps)
-    n2 = (nb[...].astype(F32) * scale2 * g2[...]).astype(BF16)
-    xb[...] = n2
-
-    outs = []
-
-    def q_piece(j):
-        return q_hbm.at[pl.ds(pl.multiple_of(own * half, half), half), pl.ds(j * QC, QC)]
-
-    def q_other(j):
-        return q_hbm.at[pl.ds(pl.multiple_of(other * half, half), half), pl.ds(j * QC, QC)]
+    nb[...] = (x2_out[...].astype(F32) * scale2 * g2[...][None, :]).astype(BF16)
+
+    def q_slot(j, kind):
+        return wgu.at[kind, 0, pl.ds(j * rows, rows), :QC]
+
+    def q_half(j, kind, h):
+        return wgu.at[kind, 0, pl.ds(pl.multiple_of(j * rows + h * half, half), half), :QC]
+
+    def q_piece(j, h):
+        return q_out.at[pl.ds(pl.multiple_of(h * half, half), half), pl.ds(j * QC, QC)]
+
+    def q_pair(j):
+        return rcopy(q_half(j, 0, other), q_half(j, 1, 0), qp_ss.at[j], qp_rs.at[j], sib)
+
+    def q_cross(j):
+        return rcopy(q_half(j, 2, 0), q_half(j, 2, 1), qs_ss.at[j], qs_rs.at[j], partner)
+
+    def q_share(j, h):
+        return rcopy(q_piece(j, h), q_piece(j, h), qo_ss.at[j], qo_rs.at[j], sib)
 
     def q_compute(j):
         wq_copy(j).wait()
-        part = dot(xb[...], wq[j]).astype(BF16)
-        qp[j, 0] = part[:half]
-        qp[j, 1] = part[half:]
-        c = rcopy(qp.at[j, other], qp_rcv.at[j], qp_ss.at[j], qp_rs.at[j], sib)
+        q_slot(j, 0)[...] = dot(nb[...], wq[j]).astype(BF16)
+        c = q_pair(j)
         c.start()
         sends.append(c)
 
     def q_sum(j):
-        rcopy(qp.at[j, other], qp_rcv.at[j], qp_ss.at[j], qp_rs.at[j], sib).wait_recv()
-        qs[j] = (qp[j, own].astype(F32) + qp_rcv[j].astype(F32)).astype(BF16)
-        c = rcopy(qs.at[j], qs_rcv.at[j], qs_ss.at[j], qs_rs.at[j], partner)
+        q_pair(j).wait_recv()
+        q_half(j, 2, 0)[...] = (q_half(j, 0, own)[...].astype(F32)
+                                + q_half(j, 1, 0)[...].astype(F32)).astype(BF16)
+        c = q_cross(j)
         c.start()
         sends.append(c)
 
     def q_final(j):
-        rcopy(qs.at[j], qs_rcv.at[j], qs_ss.at[j], qs_rs.at[j], partner).wait_recv()
-        qo[j] = (qs[j].astype(F32) + qs_rcv[j].astype(F32)).astype(BF16)
-        c = pltpu.make_async_copy(qo.at[j], q_piece(j), out_sem.at[1 + j])
-        c.start()
-        outs.append(c)
-        c = rcopy(qo.at[j], q_piece(j), qo_ss.at[j], qo_rs.at[j], sib)
+        q_cross(j).wait_recv()
+        q_piece(j, own)[...] = (q_half(j, 2, 0)[...].astype(F32)
+                                + q_half(j, 2, 1)[...].astype(F32)).astype(BF16)
+        c = q_share(j, own)
         c.start()
         sends.append(c)
 
@@ -266,10 +270,7 @@
             q_final(t - 3)
 
     for j in range(n_q):
-        rcopy(qo.at[j], q_other(j), qo_ss.at[j], qo_rs.at[j], sib).wait_recv()
-    for c in outs:
-        c.wait()
-    x2_out.wait()
+        q_share(j, other).wait_recv()
     for c in sends:
         c.wait_send()
     for c in dn_cps:
@@ -289,14 +290,13 @@
         any_spec = pl.BlockSpec(memory_space=pltpu.HBM)
         return pl.pallas_call(
             functools.partial(kernel, width * hid_ways),
-            out_shape=(jax.ShapeDtypeStruct((rows, width), BF16),
-                       jax.ShapeDtypeStruct((rows, qn), BF16)),
+            out_shape=(pltpu.VMEM((rows, width), BF16), pltpu.VMEM((rows, qn), BF16)),
             in_specs=[any_spec] * 7,
-            out_specs=(any_spec, any_spec),
+            out_specs=(pl.BlockSpec(memory_space=pltpu.VMEM),) * 2,
             scratch_shapes=[
                 pltpu.VMEM((rows, width), BF16),
-                pltpu.VMEM((1, width), F32),
-                pltpu.VMEM((1, width), F32),
+                pltpu.VMEM((width,), F32),
+                pltpu.VMEM((width,), F32),
                 pltpu.VMEM((rows, width), BF16),
                 pltpu.VMEM((SLOTS, 2, width, GC), BF16),
                 pltpu.VMEM((ff, width), BF16),
@@ -311,20 +311,15 @@
                 pltpu.VMEM((n_d, rows, DN), BF16),
                 pltpu.VMEM((2, 8, 128), F32),
                 pltpu.VMEM((2, 4, 8, 128), F32),
-                pltpu.VMEM((n_q, 2, half, QC), BF16),
-                pltpu.VMEM((n_q, half, QC), BF16),
-                pltpu.VMEM((n_q, half, QC), BF16),
-                pltpu.VMEM((n_q, half, QC), BF16),
-                pltpu.VMEM((n_q, half, QC), BF16),
-                dma((3,)), dma((n_g, 2)), dma((n_g,)), dma((n_q,)), dma((1 + n_q,)),
+                dma((3,)), dma((n_g, 2)), dma((n_g,)), dma((n_q,)),
                 dma((n_g,)), dma((n_g,)), dma((n_g,)), dma((n_g,)),
                 dma((n_g,)), dma((n_g,)), dma((n_g, 2)), dma((n_g, 2)),
                 dma((n_d,)), dma((n_d,)), dma((2, 3)), dma((2, 4)),
                 dma((n_q,)), dma((n_q,)), dma((n_q,)), dma((n_q,)), dma((n_q,)), dma((n_q,)),
             ],
             compiler_params=pltpu.CompilerParams(
-                collective_id=0, has_side_effects=True, vmem_limit_bytes=67043328),
-        )(residual, gain_mlp[None, :], gain_attn[None, :], w_gate, w_up, w_down, w_qkv)
+                collective_id=0, has_side_effects=True, vmem_limit_bytes=65400000),
+        )(residual, gain_mlp, gain_attn, w_gate, w_up, w_down, w_qkv)
 
     return jax.shard_map(
         device_step, mesh=mesh,

time: 67.1 us -> 57.3 us (0.85)
  Pallas kernels: 59.8 us -> 55 us
  local copies, waits for them, and re-layouts: 6.39 us -> 1.61 us
    pallas_call x1, Pallas kernels: 59.8 us -> 55 us  [device_step(): pl.pallas_call(functools.partial(kernel, width * hid_ways), out_shape=(pl...]
    broadcast_in_dim x2 -> x0, local copies, waits for them, and re-layouts: 2.59 us -> none  [the longest x1 1.29 us: device_step(): gain_mlp[None, :]]
    unnamed x2, local copies, waits for them, and re-layouts: 3.8 us -> 1.61 us
where the time goes in v2:
time: 57.3 us; the launch traced here: 57.2 us
  Pallas kernels  55 us (96%)
  local copies, waits for them, and re-layouts  1.61 us (3%)
  between operations  0.64 us (1%)
    pallas_call x1, Pallas kernels, device_step(): pl.pallas_call(functools.partial(kernel, width * hid_ways), out_shape=(pl...  55 us
    unnamed x2, local copies, waits for them, and re-layouts  1.61 us

profile of v2, /device:TPU:0, one launch (start us, length us, event | category | flops | bytes accessed | tf_op | source)
XLA Modules:
  0.0 57.2 jit_solution(16656731789400924147)
XLA Ops:
  0.6 55.0 %shard_map.86 = (bf16[64,1280]{1,0:T(8,128)(2,1)S(1)}, bf16[64,7680]{1,0:T(8,128)(2,1)S(1)}) custom-call(bf16[64,1280]{1,0:T(8,128)(2,1)} %x_hbm.1, f32[1280]{0:T(1024)} %g1_hbm.1, f32[1280]{0:T(1024)} %g2_hbm.1, bf16[1280,6912]{1,0:T(8,128)(2,1)} %wg_hbm.1, bf16[1280,6912]{1,0:T(8,128)(2,1)} %wu_hbm.1, bf16[6912,1280]{1,0:T(8,128)(2,1)} %wd_hbm.1, ...), custom_call_target="tpu_custom_call" | custom-call | tf_op jit(solution)/shard_map/pallas_call | solution.py:291
  55.6 0.7 %copy.11 = bf16[64,1280]{1,0:T(8,128)(2,1)} copy(bf16[64,1280]{1,0:T(8,128)(2,1)S(1)} %get-tuple-element.2) | data formatting | bytes 327680
  56.3 0.9 %copy.12 = bf16[64,7680]{1,0:T(8,128)(2,1)} copy(bf16[64,7680]{1,0:T(8,128)(2,1)S(1)} %get-tuple-element.3) | data formatting | bytes 1966080

commit v3 on v0

v3 whole, which is shorter than its diff:
```python
import functools

import jax
import jax.numpy as jnp
from jax import lax
from jax.experimental import pallas as pl
from jax.experimental.pallas import tpu as pltpu
from jax.sharding import PartitionSpec as P

NORM_EPS = 1e-6
MESH = pl.DeviceIdType.MESH
F32 = jnp.float32
BF16 = jnp.bfloat16

GROUPS = 2
CH = 768
SLOTS = 5
DN = 256
DPART = 3
NAMES = 'CSARDYXNQTF'
PARTS = (
(
    ('C', 0, 0), ('C', 0, 1), ('C', 0, 2), ('S', 0, 0), ('S', 1, 0), ('S', 0, 1), ('C', 0, 3), ('S', 0, 2),
    ('C', 0, 4), ('S', 1, 1), ('S', 0, 3), ('C', 0, 5), ('A', 0, 0), ('S', 0, 4), ('C', 0, 6), ('A', 0, 1),
    ('A', 0, 2), ('S', 0, 5), ('C', 0, 7), ('A', 0, 3), ('S', 0, 6), ('A', 1, 0), ('R', 0, 0), ('A', 1, 1),
    ('C', 0, 8),
),
(
    ('R', 0, 1), ('R', 0, 2), ('A', 0, 4), ('S', 0, 7), ('S', 1, 2), ('D', 0, 0), ('R', 0, 3), ('A', 0, 5),
    ('S', 0, 8), ('D', 0, 1), ('A', 0, 6), ('R', 1, 0), ('R', 1, 1), ('S', 1, 3), ('D', 0, 2), ('R', 0, 4),
    ('S', 1, 4), ('D', 0, 3), ('A', 0, 7), ('A', 1, 2), ('S', 1, 5), ('D', 1, 0), ('R', 0, 5), ('A', 0, 8),
    ('S', 1, 6), ('S', 1, 7), ('R', 0, 6), ('S', 1, 8), ('D', 0, 4), ('A', 1, 3), ('D', 0, 5), ('A', 1, 4),
    ('R', 0, 7), ('D', 0, 6), ('R', 1, 2), ('D', 1, 1), ('R', 0, 8), ('A', 1, 5), ('D', 0, 7), ('A', 1, 6),
    ('D', 1, 2), ('Y', 0, 8), ('R', 1, 3), ('R', 1, 4), ('R', 1, 5), ('A', 1, 7), ('A', 1, 8), ('R', 1, 6),
    ('D', 1, 3), ('D', 1, 4), ('D', 1, 5), ('R', 1, 7), ('D', 1, 6), ('R', 1, 8), ('X', 0, 0), ('D', 1, 7),
    ('Y', 1, 8), ('N', 0, 0),
),
(
    ('Q', 0, 0), ('Q', 0, 1), ('Q', 0, 2), ('T', 0, 0), ('Q', 0, 3), ('T', 0, 1), ('X', 1, 0), ('Q', 0, 4),
    ('T', 0, 2), ('Q', 0, 5), ('T', 0, 3), ('Q', 0, 6), ('T', 0, 4), ('F', 0, 0), ('Q', 0, 7), ('T', 0, 5),
    ('F', 0, 1), ('Q', 0, 8), ('N', 1, 0), ('T', 0, 6), ('T', 0, 7), ('F', 0, 2), ('F', 0, 3), ('Q', 0, 9),
    ('T', 0, 8), ('F', 0, 4), ('Q', 1, 0), ('F', 0, 5), ('Q', 1, 1), ('T', 0, 9), ('Q', 1, 2), ('T', 1, 0),
    ('F', 0, 6), ('Q', 1, 3), ('T', 1, 1), ('F', 0, 7), ('F', 0, 8), ('T', 1, 2), ('Q', 1, 4), ('Q', 1, 5),
    ('T', 1, 3), ('F', 0, 9), ('Q', 1, 6), ('T', 1, 4), ('F', 1, 0), ('Q', 1, 7), ('T', 1, 5), ('F', 1, 1),
    ('Q', 1, 8), ('T', 1, 6), ('F', 1, 2), ('Q', 1, 9), ('T', 1, 7), ('F', 1, 3), ('T', 1, 8), ('F', 1, 4),
    ('T', 1, 9), ('F', 1, 5), ('F', 1, 6), ('F', 1, 7), ('F', 1, 8), ('F', 1, 9),
),
)


def dot(a, b):
    return jnp.dot(a, b, preferred_element_type=F32)


def add(a, b):
    return (a.astype(F32) + b.astype(F32)).astype(BF16)


def kernel(d_model, x_hbm, g1_hbm, g2_hbm, wg_hbm, wu_hbm, wd_hbm, wq_hbm, x2_out, q_out,
           xb, g1, g2, nb, wgu, wd, wq, p_buf, p_rcv, s_buf, s_rcv, a_buf, acc,
           dn_snd, dn_rcv, st_snd, st_rcv,
           in_sem, wgu_sem, wd_sem, wq_sem, sent, pair_rs, cross_rs, share_rs, ad_rs, dn_rs, st_rs):
    rows, width = nb.shape
    gr = rows // GROUPS
    qr = gr // 2
    n_g, n_q, n_d = wg_hbm.shape[1] // CH, wq_hbm.shape[1] // CH, width // DN
    hc = CH // 2

    me = lax.axis_index('hid')
    y = lax.axis_index('ffn')
    z = lax.axis_index('data')
    chip = me // 2
    core = me % 2
    own = (core + chip) % 2
    other = 1 - own
    sib = (z, y, chip * 2 + (1 - core))
    partner = (z, y, (1 - chip) * 2 + (1 - core))
    ypeer = (z, 1 - y, me)
    hid_peers = [(z, y, (me + k) % 4) for k in (1, 2, 3)]

    def rcopy(src, dst, ss, rs, dev):
        return pltpu.make_async_remote_copy(src_ref=src, dst_ref=dst, send_sem=ss, recv_sem=rs,
                                            device_id=dev, device_id_type=MESH)

    def span(start, n):
        return pl.ds(pl.multiple_of(start, n), n)

    def each(n, body):
        @pl.loop(0, n)
        def _(i):
            body(i)

    def gu_copy(j, i):
        w = (wg_hbm, wu_hbm)[i]
        return pltpu.make_async_copy(w.at[:, span(j * CH, CH)], wgu.at[j % SLOTS, i], wgu_sem.at[j % SLOTS])

    def gu_wait(j):
        slot = wgu.at[j % SLOTS]
        pltpu.make_async_copy(slot, slot, wgu_sem.at[j % SLOTS]).wait()

    def wd_copy(p):
        r = span(p * DPART * CH, DPART * CH)
        return pltpu.make_async_copy(wd_hbm.at[r, :], wd.at[r, :], wd_sem.at[p])

    def wq_copy(j):
        return pltpu.make_async_copy(wq_hbm.at[:, span(j * CH, CH)], wq.at[j], wq_sem.at[j])

    def natural(g, h):
        return h * (rows // 2) + g * qr

    def held(g, h):
        return span(g * gr + h * qr, qr)

    for g in range(GROUPS):
        for h in range(2):
            pltpu.make_async_copy(x_hbm.at[pl.ds(natural(g, h), qr)],
                                  xb.at[pl.ds(g * gr + h * qr, qr)], in_sem.at[0]).start()
    gains = [pltpu.make_async_copy(s, d, in_sem.at[1 + i])
             for i, (s, d) in enumerate(((g1_hbm, g1), (g2_hbm, g2)))]
    for c in gains:
        c.start()
    for j in range(SLOTS):
        for i in range(2):
            gu_copy(j, i).start(priority=1)

    barrier = pltpu.get_barrier_semaphore()
    for dev in hid_peers + [ypeer]:
        pl.semaphore_signal(barrier, inc=1, device_id=dev, device_id_type=MESH)

    def stat_store(t, sq):
        cols = jnp.sum(sq.T, axis=0, keepdims=True)
        cols = jnp.concatenate([cols] * (128 // cols.shape[1]), axis=1)
        st_snd[t] = jnp.broadcast_to(cols, (8, 128))

    def stat_copy(t, k):
        return rcopy(st_snd.at[t], st_rcv.at[t, k], sent.at[0], st_rs.at[t], hid_peers[k])

    def stat_scale(t, n):
        pltpu.make_async_copy(st_rcv.at[t], st_rcv.at[t], st_rs.at[t]).wait()
        total = (st_snd[t] + st_rcv[t, 0]) + (st_rcv[t, 1] + st_rcv[t, 2])
        return lax.rsqrt(total / d_model + NORM_EPS).T[:n, 0:1]

    def lane_sq(v):
        out = None
        for k in range(v.shape[1] // 128):
            t = v[:, k * 128:(k + 1) * 128]
            out = t * t if out is None else out + t * t
        return out

    pltpu.make_async_copy(xb, xb, in_sem.at[0]).wait()
    for c in gains:
        c.wait()
    stat_store(0, lane_sq(xb[...].astype(F32)))
    pl.semaphore_wait(barrier, 4)
    for k in range(3):
        stat_copy(0, k).start()
    scale1 = stat_scale(0, rows)
    nb[...] = (xb[...].astype(F32) * scale1 * g1[...][None, :]).astype(BF16)

    def p_copy(g, j):
        c = span(j * CH, CH)
        return rcopy(p_buf.at[:, held(g, other), c], p_rcv.at[:, span(g * qr, qr), c],
                     sent.at[1], pair_rs.at[g, j], sib)

    def s_copy(g, j):
        r = span(g * qr, qr)
        return rcopy(s_buf.at[:, r, span(j * CH + (1 - chip) * hc, hc)], s_rcv.at[:, r, span(j * hc, hc)],
                     sent.at[2], cross_rs.at[g, j], partner)

    def a_piece(g, j, h, ch):
        return a_buf.at[g, span(h * qr, qr), span(j * CH + ch * hc, hc)]

    def ax_copy(g, j, ch):
        piece = a_piece(g, j, own, ch)
        return rcopy(piece, piece, sent.at[3], share_rs.at[g, j], partner)

    def ad_copy(g, j, ch):
        piece = a_piece(g, j, own, ch)
        return rcopy(piece, piece, sent.at[4], ad_rs.at[g, j], sib)

    def do_c(_, j):
        c = span(j * CH, CH)
        gu_wait(j)

        def one(i):
            p_buf[i, :, c] = dot(nb[...], wgu[j % SLOTS, i]).astype(BF16)
        each(2, one)
        for g in range(GROUPS):
            p_copy(g, j).start()

        @pl.when(j + SLOTS < n_g)
        def _():
            for i in range(2):
                gu_copy(j + SLOTS, i).start(priority=1)

        @pl.when(j + SLOTS == n_g - 1)
        def _():
            each(n_g // DPART, lambda k: wd_copy(k).start(priority=1))
            each(n_q, lambda k: wq_copy(k).start(priority=1))

    def do_s(g, j):
        p_copy(g, j).wait_recv()
        r = span(g * qr, qr)
        c = span(j * CH, CH)
        s_buf[:, r, c] = add(p_buf[:, held(g, own), c], p_rcv[:, r, c])
        s_copy(g, j).start()

    def do_a(g, j):
        s_copy(g, j).wait_recv()
        r = span(g * qr, qr)
        gu = add(s_buf[:, r, span(j * CH + chip * hc, hc)], s_rcv[:, r, span(j * hc, hc)]).astype(F32)
        a_buf[g, span(own * qr, qr), span(j * CH + chip * hc, hc)] = (jax.nn.silu(gu[0]) * gu[1]).astype(BF16)
        ax_copy(g, j, chip).start()
        ad_copy(g, j, chip).start()

    def do_r(g, j):
        ax_copy(g, j, 1 - chip).wait_recv()
        ad_copy(g, j, 1 - chip).start()

    def down_operands(g, j):
        got = a_buf.at[g, span(other * qr, qr), span(j * CH, CH)]
        pltpu.make_async_copy(got, got, ad_rs.at[g, j]).wait()

        @pl.when((g == 0) & (j % DPART == 0))
        def _():
            wd_copy(j // DPART).wait()

    def do_d(g, j):
        down_operands(g, j)
        k = span(j * CH, CH)
        old = jnp.where(j == 0, 0.0, acc[g])
        acc[g] = old + dot(a_buf[g, :, k], wd[k, :])

    def dn_copy(g, n):
        return rcopy(dn_snd.at[g, n], dn_rcv.at[g, n], sent.at[5], dn_rs.at[g], ypeer)

    def do_y(g, j):
        down_operands(g, j)
        k = span(j * CH, CH)

        def piece(n):
            c = span(n * DN, DN)
            dn_snd[g, n] = (acc[g, :, c] + dot(a_buf[g, :, k], wd[k, c])).astype(BF16)
            dn_copy(g, n).start()
        each(n_d, piece)

    def do_x(g, _):
        sq = None
        r = span(g * gr, gr)
        pltpu.make_async_copy(dn_rcv.at[g], dn_rcv.at[g], dn_rs.at[g]).wait()
        for n in range(n_d):
            c = pl.ds(n * DN, DN)
            x2 = add(xb[r, c], add(dn_snd[g, n], dn_rcv[g, n]))
            xb[r, c] = x2
            for h in range(2):
                x2_out[span(natural(g, h), qr), c] = x2[h * qr:(h + 1) * qr]
            s = lane_sq(x2.astype(F32))
            sq = s if sq is None else sq + s
        stat_store(1 + g, sq)
        for k in range(3):
            stat_copy(1 + g, k).start()

    def do_n(g, _):
        r = span(g * gr, gr)
        scale = stat_scale(1 + g, gr)
        nb[r] = (xb[r].astype(F32) * scale * g2[...][None, :]).astype(BF16)

    def qp_ref(g, j, h):
        return wgu.at[0, 0, span(j * rows + g * gr + h * qr, qr)]

    def q_ref(kind, g, j):
        return wgu.at[kind, 0, span(j * gr + g * qr, qr)]

    def q_piece(g, j, h):
        return q_out.at[span(natural(g, h), qr), span(j * CH, CH)]

    def qp_copy(g, j):
        return rcopy(qp_ref(g, j, other), q_ref(1, g, j), sent.at[6], pair_rs.at[g, j], sib)

    def qs_copy(g, j):
        return rcopy(q_ref(2, g, j), q_ref(3, g, j), sent.at[7], cross_rs.at[g, j], partner)

    def qo_copy(g, j, h):
        return rcopy(q_piece(g, j, h), q_piece(g, j, h), sent.at[8], share_rs.at[g, j], sib)

    def do_q(g, j):
        @pl.when(g == 0)
        def _():
            wq_copy(j).wait()
        wgu[0, 0, span(j * rows + g * gr, gr)] = dot(nb[span(g * gr, gr)], wq[j]).astype(BF16)
        qp_copy(g, j).start()

    def do_t(g, j):
        qp_copy(g, j).wait_recv()
        q_ref(2, g, j)[...] = add(qp_ref(g, j, own)[...], q_ref(1, g, j)[...])
        qs_copy(g, j).start()

    def do_f(g, j):
        qs_copy(g, j).wait_recv()
        q_piece(g, j, own)[...] = add(q_ref(2, g, j)[...], q_ref(3, g, j)[...])
        qo_copy(g, j, own).start()

    tasks = dict(C=do_c, S=do_s, A=do_a, R=do_r, D=do_d, Y=do_y, X=do_x, N=do_n, Q=do_q, T=do_t, F=do_f)

    def run(kinds, kind, g, j):
        if len(kinds) == 1:
            if kinds[0] < len(NAMES):
                tasks[NAMES[kinds[0]]](g, j)
            return
        low, high = kinds[:len(kinds) // 2], kinds[len(kinds) // 2:]
        lax.cond(kind < high[0], lambda: run(low, kind, g, j), lambda: run(high, kind, g, j))

    for part in PARTS:
        codes = [NAMES.index(name) * 32 + g * 16 + j for name, g, j in part]
        codes += [len(NAMES) * 32] * (-len(codes) % 3)
        kinds = sorted({c // 32 for c in codes})
        words = [codes[i] + codes[i + 1] * 512 + codes[i + 2] * 512 * 512 for i in range(0, len(codes), 3)]

        @pl.loop(0, len(words))
        def _(i):
            word = jnp.int32(words[0])
            for n, w in enumerate(words):
                word = jnp.where(i == n, jnp.int32(w), word)

            def step(_, word):
                code = lax.rem(word, jnp.int32(512))
                gj = lax.rem(code, jnp.int32(32))
                run(kinds, lax.div(code, jnp.int32(32)), lax.div(gj, jnp.int32(16)), lax.rem(gj, jnp.int32(16)))
                return lax.div(word, jnp.int32(512))
            lax.fori_loop(0, 3, step, word)

    for g in range(GROUPS):
        each(n_q, lambda j: qo_copy(g, j, other).wait_recv())
    a_half = a_buf.at[:, :qr]
    q_part = wgu.at[1, 0, pl.ds(0, n_q * gr)]
    for i, ref in enumerate((st_rcv, p_rcv, s_rcv, a_buf.at[:, :qr, :n_g * hc], a_half, dn_rcv,
                             q_part, q_part, q_out.at[:rows // 2])):
        pltpu.make_async_copy(ref, ref, sent.at[i]).wait()


def solution(mesh):
    hid_ways = mesh.shape['hid']

    def device_step(residual, gain_mlp, gain_attn, w_gate, w_up, w_down, w_qkv):
        rows, width = residual.shape
        ff = w_gate.shape[1]
        qn = w_qkv.shape[1]
        half = rows // 2
        gr = rows // GROUPS
        n_g, n_q, n_d = ff // CH, qn // CH, width // DN
        dma = pltpu.SemaphoreType.DMA
        gg, gq = dma((GROUPS, n_g)), dma((GROUPS, n_q))
        return pl.pallas_call(
            functools.partial(kernel, width * hid_ways),
            out_shape=(pltpu.VMEM((rows, width), BF16), pltpu.VMEM((rows, qn), BF16)),
            in_specs=[pl.BlockSpec(memory_space=pltpu.HBM)] * 7,
            out_specs=(pl.BlockSpec(memory_space=pltpu.VMEM),) * 2,
            scratch_shapes=[
                pltpu.VMEM((rows, width), BF16),
                pltpu.VMEM((width,), F32),
                pltpu.VMEM((width,), F32),
                pltpu.VMEM((rows, width), BF16),
                pltpu.VMEM((SLOTS, 2, width, CH), BF16),
                pltpu.VMEM((ff, width), BF16),
                pltpu.VMEM((n_q, width, CH), BF16),
                pltpu.VMEM((2, rows, ff), BF16),
                pltpu.VMEM((2, half, ff), BF16),
                pltpu.VMEM((2, half, ff), BF16),
                pltpu.VMEM((2, half, ff // 2), BF16),
                pltpu.VMEM((GROUPS, gr, ff), BF16),
                pltpu.VMEM((GROUPS, gr, width), F32),
                pltpu.VMEM((GROUPS, n_d, gr, DN), BF16),
                pltpu.VMEM((GROUPS, n_d, gr, DN), BF16),
                pltpu.VMEM((1 + GROUPS, 8, 128), F32),
                pltpu.VMEM((1 + GROUPS, 3, 8, 128), F32),
                dma((3,)), dma((SLOTS,)), dma((n_g // DPART,)), dma((n_q,)), dma((9,)),
                gq, gq, gq, gg, dma((GROUPS,)), dma((1 + GROUPS,)),
            ],
            compiler_params=pltpu.CompilerParams(
                collective_id=0, has_side_effects=True, vmem_limit_bytes=65400000),
        )(residual, gain_mlp, gain_attn, w_gate, w_up, w_down, w_qkv)

    return jax.shard_map(
        device_step, mesh=mesh,
        in_specs=(P('data', 'hid'), P('hid'), P('hid'), P('hid', 'ffn'), P('hid', 'ffn'),
                  P('ffn', 'hid'), P('hid', 'ffn')),
        out_specs=(P('data', 'hid'), P('data', 'ffn')),
        check_vma=False)
```

time: 158 us -> 52.7 us (0.33)
  waiting for transfers between devices: 87.4 us -> 0 us
  Pallas kernels: 0 us -> 50.4 us
  matrix products: 36.1 us -> 0 us
  blocking collectives: 14.8 us -> 0 us
  between operations: 13.8 us -> 0.64 us
  other arithmetic: 2.17 us -> 0 us
  local copies, waits for them, and re-layouts: 3.23 us -> 1.61 us
    psum x3 -> x0, waiting for transfers between devices: 87.3 us -> none  [the longest x1 40.5 us: device_step(): gate_sum, up_sum = lax.psum((gate_part, up_part), 'hid')]
    pallas_call x0 -> x1, Pallas kernels: none -> 50.4 us  [device_step(): pl.pallas_call(functools.partial(kernel, width * hid_ways), out_shape=(pl...]
    dot_general x4 -> x0, matrix products: 36.1 us -> none  [the longest x1 11.2 us: device_step(): jnp.dot(normed_next, w_qkv, preferred_element_type=jnp.float32)]
    psum x2 -> x0, blocking collectives: 14.8 us -> none  [shard_norm(): full_sq = lax.psum(part_sq, 'hid')]
    reduce_sum x2 -> x0, other arithmetic: 2.15 us -> none  [shard_norm(): part_sq = jnp.sum(resid32 * resid32, axis=1, keepdims=True)]
    unnamed x11 -> x2, local copies, waits for them, and re-layouts: 3.23 us -> 1.61 us
  transfers between devices with their start and end apart: 3 -> 0, of which waited for: 3 -> 0; matrix products, arithmetic and copies ran while one was open for 0% -> 0% of each run, Pallas kernels for 0% -> 0%
where the time goes in v3:
time: 52.7 us; the launch traced here: 52.6 us
  Pallas kernels  50.4 us (96%)
  local copies, waits for them, and re-layouts  1.61 us (3%)
  between operations  0.64 us (1%)
    pallas_call x1, Pallas kernels, device_step(): pl.pallas_call(functools.partial(kernel, width * hid_ways), out_shape=(pl...  50.4 us
    unnamed x2, local copies, waits for them, and re-layouts  1.61 us

profile of v3, /device:TPU:0, one launch (start us, length us, event | category | flops | bytes accessed | tf_op | source)
XLA Modules:
  0.0 52.6 jit_solution(8280615035895290913)
XLA Ops:
  0.6 50.4 %shard_map.86 = (bf16[64,1280]{1,0:T(8,128)(2,1)S(1)}, bf16[64,7680]{1,0:T(8,128)(2,1)S(1)}) custom-call(bf16[64,1280]{1,0:T(8,128)(2,1)} %x_hbm.1, f32[1280]{0:T(1024)} %g1_hbm.1, f32[1280]{0:T(1024)} %g2_hbm.1, bf16[1280,6912]{1,0:T(8,128)(2,1)} %wg_hbm.1, bf16[1280,6912]{1,0:T(8,128)(2,1)} %wu_hbm.1, bf16[6912,1280]{1,0:T(8,128)(2,1)} %wd_hbm.1, ...), custom_call_target="tpu_custom_call" | custom-call | tf_op jit(solution)/shard_map/pallas_call | solution.py:353
  51.0 0.7 %copy.11 = bf16[64,1280]{1,0:T(8,128)(2,1)} copy(bf16[64,1280]{1,0:T(8,128)(2,1)S(1)} %get-tuple-element.2) | data formatting | bytes 327680
  51.7 0.9 %copy.12 = bf16[64,7680]{1,0:T(8,128)(2,1)} copy(bf16[64,7680]{1,0:T(8,128)(2,1)S(1)} %get-tuple-element.3) | data formatting | bytes 1966080

commit v4 on v3

--- a/solution.py
+++ b/solution.py
@@ -8,6 +8,8 @@
 from jax.sharding import PartitionSpec as P
 
 NORM_EPS = 1e-6
+LEAST = 1e-30
+SHRINK = 2048.0
 MESH = pl.DeviceIdType.MESH
 F32 = jnp.float32
 BF16 = jnp.bfloat16
@@ -17,33 +19,32 @@
 SLOTS = 5
 DN = 256
 DPART = 3
-NAMES = 'CSARDYXNQTF'
+NAMES = 'CSARDYXNQTFZB'
 PARTS = (
 (
-    ('C', 0, 0), ('C', 0, 1), ('C', 0, 2), ('S', 0, 0), ('S', 1, 0), ('S', 0, 1), ('C', 0, 3), ('S', 0, 2),
-    ('C', 0, 4), ('S', 1, 1), ('S', 0, 3), ('C', 0, 5), ('A', 0, 0), ('S', 0, 4), ('C', 0, 6), ('A', 0, 1),
-    ('A', 0, 2), ('S', 0, 5), ('C', 0, 7), ('A', 0, 3), ('S', 0, 6), ('A', 1, 0), ('R', 0, 0), ('A', 1, 1),
-    ('C', 0, 8),
+    ('C', 0, 0), ('C', 0, 1), ('C', 0, 2), ('Z', 0, 0), ('S', 0, 0), ('S', 0, 1), ('S', 1, 0), ('C', 0, 3),
+    ('S', 0, 2), ('S', 1, 1), ('C', 0, 4), ('S', 0, 3), ('S', 1, 2), ('A', 0, 0), ('C', 0, 5), ('A', 0, 1),
+    ('S', 0, 4), ('C', 0, 6), ('A', 0, 2), ('S', 0, 5), ('A', 1, 0), ('C', 0, 7), ('A', 0, 3), ('S', 0, 6),
+    ('A', 1, 1), ('R', 0, 0), ('A', 1, 2), ('C', 0, 8),
 ),
 (
-    ('R', 0, 1), ('R', 0, 2), ('A', 0, 4), ('S', 0, 7), ('S', 1, 2), ('D', 0, 0), ('R', 0, 3), ('A', 0, 5),
-    ('S', 0, 8), ('D', 0, 1), ('A', 0, 6), ('R', 1, 0), ('R', 1, 1), ('S', 1, 3), ('D', 0, 2), ('R', 0, 4),
-    ('S', 1, 4), ('D', 0, 3), ('A', 0, 7), ('A', 1, 2), ('S', 1, 5), ('D', 1, 0), ('R', 0, 5), ('A', 0, 8),
-    ('S', 1, 6), ('S', 1, 7), ('R', 0, 6), ('S', 1, 8), ('D', 0, 4), ('A', 1, 3), ('D', 0, 5), ('A', 1, 4),
-    ('R', 0, 7), ('D', 0, 6), ('R', 1, 2), ('D', 1, 1), ('R', 0, 8), ('A', 1, 5), ('D', 0, 7), ('A', 1, 6),
-    ('D', 1, 2), ('Y', 0, 8), ('R', 1, 3), ('R', 1, 4), ('R', 1, 5), ('A', 1, 7), ('A', 1, 8), ('R', 1, 6),
-    ('D', 1, 3), ('D', 1, 4), ('D', 1, 5), ('R', 1, 7), ('D', 1, 6), ('R', 1, 8), ('X', 0, 0), ('D', 1, 7),
-    ('Y', 1, 8), ('N', 0, 0),
+    ('R', 0, 1), ('A', 0, 4), ('R', 0, 2), ('S', 0, 7), ('S', 1, 3), ('S', 1, 4), ('A', 0, 5), ('D', 0, 0),
+    ('R', 0, 3), ('S', 0, 8), ('R', 1, 0), ('D', 0, 1), ('A', 0, 6), ('R', 1, 1), ('R', 1, 2), ('S', 1, 5),
+    ('D', 0, 2), ('R', 0, 4), ('S', 1, 6), ('A', 0, 7), ('D', 0, 3), ('A', 1, 3), ('S', 1, 7), ('D', 0, 4),
+    ('R', 0, 5), ('A', 1, 4), ('D', 1, 0), ('A', 0, 8), ('R', 0, 6), ('S', 1, 8), ('D', 1, 1), ('A', 1, 5),
+    ('D', 0, 5), ('R', 0, 7), ('A', 1, 6), ('D', 0, 6), ('R', 1, 3), ('D', 1, 2), ('R', 1, 4), ('A', 1, 7),
+    ('R', 0, 8), ('D', 0, 7), ('A', 1, 8), ('D', 1, 3), ('Y', 0, 8), ('R', 1, 5), ('R', 1, 6), ('R', 1, 7),
+    ('D', 1, 4), ('R', 1, 8), ('D', 1, 5), ('D', 1, 6), ('D', 1, 7), ('Y', 1, 8),
 ),
 (
-    ('Q', 0, 0), ('Q', 0, 1), ('Q', 0, 2), ('T', 0, 0), ('Q', 0, 3), ('T', 0, 1), ('X', 1, 0), ('Q', 0, 4),
-    ('T', 0, 2), ('Q', 0, 5), ('T', 0, 3), ('Q', 0, 6), ('T', 0, 4), ('F', 0, 0), ('Q', 0, 7), ('T', 0, 5),
-    ('F', 0, 1), ('Q', 0, 8), ('N', 1, 0), ('T', 0, 6), ('T', 0, 7), ('F', 0, 2), ('F', 0, 3), ('Q', 0, 9),
-    ('T', 0, 8), ('F', 0, 4), ('Q', 1, 0), ('F', 0, 5), ('Q', 1, 1), ('T', 0, 9), ('Q', 1, 2), ('T', 1, 0),
-    ('F', 0, 6), ('Q', 1, 3), ('T', 1, 1), ('F', 0, 7), ('F', 0, 8), ('T', 1, 2), ('Q', 1, 4), ('Q', 1, 5),
-    ('T', 1, 3), ('F', 0, 9), ('Q', 1, 6), ('T', 1, 4), ('F', 1, 0), ('Q', 1, 7), ('T', 1, 5), ('F', 1, 1),
-    ('Q', 1, 8), ('T', 1, 6), ('F', 1, 2), ('Q', 1, 9), ('T', 1, 7), ('F', 1, 3), ('T', 1, 8), ('F', 1, 4),
-    ('T', 1, 9), ('F', 1, 5), ('F', 1, 6), ('F', 1, 7), ('F', 1, 8), ('F', 1, 9),
+    ('X', 0, 0), ('Q', 0, 0), ('Q', 0, 1), ('Q', 0, 2), ('Q', 0, 3), ('Q', 0, 4), ('N', 0, 0), ('T', 0, 0),
+    ('T', 0, 1), ('X', 1, 0), ('T', 0, 2), ('T', 0, 3), ('Q', 0, 5), ('T', 0, 4), ('B', 0, 6), ('B', 0, 7),
+    ('T', 0, 5), ('F', 0, 0), ('B', 0, 8), ('T', 0, 6), ('F', 0, 1), ('N', 1, 0), ('T', 0, 7), ('T', 1, 6),
+    ('T', 1, 7), ('F', 0, 2), ('B', 0, 9), ('T', 0, 8), ('T', 1, 8), ('F', 0, 3), ('Q', 1, 0), ('F', 0, 4),
+    ('Q', 1, 1), ('T', 0, 9), ('T', 1, 9), ('F', 0, 5), ('F', 0, 6), ('Q', 1, 2), ('T', 1, 0), ('F', 0, 7),
+    ('T', 1, 1), ('Q', 1, 3), ('F', 1, 6), ('Q', 1, 4), ('T', 1, 2), ('F', 1, 7), ('F', 0, 8), ('Q', 1, 5),
+    ('T', 1, 3), ('F', 1, 8), ('T', 1, 4), ('F', 0, 9), ('T', 1, 5), ('F', 1, 9), ('F', 1, 0), ('F', 1, 1),
+    ('F', 1, 2), ('F', 1, 3), ('F', 1, 4), ('F', 1, 5),
 ),
 )
 
@@ -57,7 +58,7 @@
 
 
 def kernel(d_model, x_hbm, g1_hbm, g2_hbm, wg_hbm, wu_hbm, wd_hbm, wq_hbm, x2_out, q_out,
-           xb, g1, g2, nb, wgu, wd, wq, p_buf, p_rcv, s_buf, s_rcv, a_buf, acc,
+           xb, g1, g2, nb, fac, wgu, wd, wq, p_buf, p_rcv, s_buf, s_rcv, a_buf, acc,
            dn_snd, dn_rcv, st_snd, st_rcv,
            in_sem, wgu_sem, wd_sem, wq_sem, sent, pair_rs, cross_rs, share_rs, ad_rs, dn_rs, st_rs):
     rows, width = nb.shape
@@ -127,35 +128,59 @@
     for dev in hid_peers + [ypeer]:
         pl.semaphore_signal(barrier, inc=1, device_id=dev, device_id_type=MESH)
 
-    def stat_store(t, sq):
-        cols = jnp.sum(sq.T, axis=0, keepdims=True)
-        cols = jnp.concatenate([cols] * (128 // cols.shape[1]), axis=1)
-        st_snd[t] = jnp.broadcast_to(cols, (8, 128))
+    lane_row = lax.broadcasted_iota(jnp.int32, (8, 128), 0)
+
+    def gain_max(g):
+        return jnp.maximum(jnp.max(jnp.abs(g[...][None, :]), axis=1, keepdims=True), LEAST)
+
+    def normalise(t, r, n, g):
+        x = xb[r].astype(F32)
+        sq = top = None
+        for k in range(width // 128):
+            p = x[:, k * 128:(k + 1) * 128]
+            sq = p * p if sq is None else sq + p * p
+            top = jnp.abs(p) if top is None else jnp.maximum(top, jnp.abs(p))
+        sums = jnp.sum(sq.T, axis=0, keepdims=True)
+        tops = jnp.maximum(jnp.max(top.T, axis=0, keepdims=True), LEAST)
+        sums, tops = [jnp.concatenate([v] * (128 // n), axis=1) for v in (sums, tops)]
+        v = gain_max(g)
+        st_snd[t] = jnp.where(lane_row == 0, sums, jnp.where(lane_row == 1, tops, v))
+        u = jnp.maximum(jnp.max(top, axis=1, keepdims=True), LEAST)
+        gain = g[...][None, :] / v / SHRINK
+        nb[r] = (x * (1.0 / u) * gain).astype(BF16)
 
     def stat_copy(t, k):
         return rcopy(st_snd.at[t], st_rcv.at[t, k], sent.at[0], st_rs.at[t], hid_peers[k])
 
-    def stat_scale(t, n):
+    def stat_factors(t, which, r, n):
         pltpu.make_async_copy(st_rcv.at[t], st_rcv.at[t], st_rs.at[t]).wait()
         total = (st_snd[t] + st_rcv[t, 0]) + (st_rcv[t, 1] + st_rcv[t, 2])
-        return lax.rsqrt(total / d_model + NORM_EPS).T[:n, 0:1]
-
-    def lane_sq(v):
-        out = None
-        for k in range(v.shape[1] // 128):
-            t = v[:, k * 128:(k + 1) * 128]
-            out = t * t if out is None else out + t * t
-        return out
+        scale = lax.rsqrt(total[0:1] / d_model + NORM_EPS)
+        rows_ = []
+        for msg in (st_snd[t], st_rcv[t, 2 * (1 - core)]):
+            v = msg[2:3]
+            rows_.append((scale * msg[1:2] * SHRINK) * jnp.minimum(v, 1.0))
+            rows_.append(jnp.maximum(v, 1.0))
+        packed = rows_[3]
+        for k in range(3):
+            packed = jnp.where(lane_row == k, rows_[k], packed)
+        cols = packed.T
+        for k in range(4):
+            fac[which, k, r] = jnp.broadcast_to(cols[:n, k:k + 1], (n, 128))
+
+    def pair_add(which, r, mine, theirs):
+        def scaled(v, k):
+            f = [jnp.concatenate([fac[which, 2 * k + i, r]] * (CH // 128), axis=1) for i in range(2)]
+            return v.astype(F32) * f[0] * f[1]
+        return (scaled(mine, 0) + scaled(theirs, 1)).astype(BF16)
 
     pltpu.make_async_copy(xb, xb, in_sem.at[0]).wait()
     for c in gains:
         c.wait()
-    stat_store(0, lane_sq(xb[...].astype(F32)))
+    normalise(0, pl.ds(0, rows), rows, g1)
     pl.semaphore_wait(barrier, 4)
     for k in range(3):
         stat_copy(0, k).start()
-    scale1 = stat_scale(0, rows)
-    nb[...] = (xb[...].astype(F32) * scale1 * g1[...][None, :]).astype(BF16)
 
     def p_copy(g, j):
         c = span(j * CH, CH)
@@ -202,7 +227,8 @@
         p_copy(g, j).wait_recv()
         r = span(g * qr, qr)
         c = span(j * CH, CH)
-        s_buf[:, r, c] = add(p_buf[:, held(g, own), c], p_rcv[:, r, c])
+        rr = held(g, own)
+        s_buf[:, r, c] = pair_add(0, rr, p_buf[:, rr, c], p_rcv[:, r, c])
         s_copy(g, j).start()
 
     def do_a(g, j):
@@ -245,7 +271,6 @@
         each(n_d, piece)
 
     def do_x(g, _):
-        sq = None
         r = span(g * gr, gr)
         pltpu.make_async_copy(dn_rcv.at[g], dn_rcv.at[g], dn_rs.at[g]).wait()
         for n in range(n_d):
@@ -254,16 +279,15 @@
             xb[r, c] = x2
             for h in range(2):
                 x2_out[span(natural(g, h), qr), c] = x2[h * qr:(h + 1) * qr]
-            s = lane_sq(x2.astype(F32))
-            sq = s if sq is None else sq + s
-        stat_store(1 + g, sq)
+        normalise(1 + g, r, gr, g2)
         for k in range(3):
             stat_copy(1 + g, k).start()
 
     def do_n(g, _):
-        r = span(g * gr, gr)
-        scale = stat_scale(1 + g, gr)
-        nb[r] = (xb[r].astype(F32) * scale * g2[...][None, :]).astype(BF16)
+        stat_factors(1 + g, 1, span(g * gr, gr), gr)
+
+    def do_z(_, __):
+        stat_factors(0, 0, pl.ds(0, rows), rows)
 
     def qp_ref(g, j, h):
         return wgu.at[0, 0, span(j * rows + g * gr + h * qr, qr)]
@@ -290,9 +314,15 @@
         wgu[0, 0, span(j * rows + g * gr, gr)] = dot(nb[span(g * gr, gr)], wq[j]).astype(BF16)
         qp_copy(g, j).start()
 
+    def do_b(_, j):
+        wq_copy(j).wait()
+        wgu[0, 0, span(j * rows, rows)] = dot(nb[...], wq[j]).astype(BF16)
+        for g in range(GROUPS):
+            qp_copy(g, j).start()
+
     def do_t(g, j):
         qp_copy(g, j).wait_recv()
-        q_ref(2, g, j)[...] = add(qp_ref(g, j, own)[...], q_ref(1, g, j)[...])
+        q_ref(2, g, j)[...] = pair_add(1, held(g, own), qp_ref(g, j, own)[...], q_ref(1, g, j)[...])
         qs_copy(g, j).start()
 
     def do_f(g, j):
@@ -300,7 +330,8 @@
         q_piece(g, j, own)[...] = add(q_ref(2, g, j)[...], q_ref(3, g, j)[...])
         qo_copy(g, j, own).start()
 
-    tasks = dict(C=do_c, S=do_s, A=do_a, R=do_r, D=do_d, Y=do_y, X=do_x, N=do_n, Q=do_q, T=do_t, F=do_f)
+    tasks = dict(C=do_c, S=do_s, A=do_a, R=do_r, D=do_d, Y=do_y, X=do_x, N=do_n, Q=do_q, T=do_t, F=do_f,
+                 Z=do_z, B=do_b)
 
     def run(kinds, kind, g, j):
         if len(kinds) == 1:
@@ -360,6 +391,7 @@
                 pltpu.VMEM((width,), F32),
                 pltpu.VMEM((width,), F32),
                 pltpu.VMEM((rows, width), BF16),
+                pltpu.VMEM((2, 4, rows, 128), F32),
                 pltpu.VMEM((SLOTS, 2, width, CH), BF16),
                 pltpu.VMEM((ff, width), BF16),
                 pltpu.VMEM((n_q, width, CH), BF16),

time: 52.7 us -> 48.7 us (0.924)
  Pallas kernels: 50.4 us -> 46.4 us
    pallas_call x1, Pallas kernels: 50.4 us -> 46.4 us  [device_step(): pl.pallas_call(functools.partial(kernel, width * hid_ways), out_shape=(pl...]
where the time goes in v4:
time: 48.7 us; the launch traced here: 48.6 us
  Pallas kernels  46.4 us (95%)
  local copies, waits for them, and re-layouts  1.61 us (3%)
  between operations  0.64 us (1%)
    pallas_call x1, Pallas kernels, device_step(): pl.pallas_call(functools.partial(kernel, width * hid_ways), out_shape=(pl...  46.4 us
    unnamed x2, local copies, waits for them, and re-layouts  1.61 us

profile of v4, /device:TPU:0, one launch (start us, length us, event | category | flops | bytes accessed | tf_op | source)
XLA Modules:
  0.0 48.6 jit_solution(67613833296460426)
XLA Ops:
  0.6 46.4 %shard_map.86 = (bf16[64,1280]{1,0:T(8,128)(2,1)S(1)}, bf16[64,7680]{1,0:T(8,128)(2,1)S(1)}) custom-call(bf16[64,1280]{1,0:T(8,128)(2,1)} %x_hbm.1, f32[1280]{0:T(1024)} %g1_hbm.1, f32[1280]{0:T(1024)} %g2_hbm.1, bf16[1280,6912]{1,0:T(8,128)(2,1)} %wg_hbm.1, bf16[1280,6912]{1,0:T(8,128)(2,1)} %wu_hbm.1, bf16[6912,1280]{1,0:T(8,128)(2,1)} %wd_hbm.1, ...), custom_call_target="tpu_custom_call" | custom-call | tf_op jit(solution)/shard_map/pallas_call | solution.py:384
  47.0 0.7 %copy.11 = bf16[64,1280]{1,0:T(8,128)(2,1)} copy(bf16[64,1280]{1,0:T(8,128)(2,1)S(1)} %get-tuple-element.2) | data formatting | bytes 327680
  47.7 0.9 %copy.12 = bf16[64,7680]{1,0:T(8,128)(2,1)} copy(bf16[64,7680]{1,0:T(8,128)(2,1)S(1)} %get-tuple-element.3) | data formatting | bytes 1966080

commit v5 on v4

--- a/solution.py
+++ b/solution.py
@@ -9,7 +9,7 @@
 
 NORM_EPS = 1e-6
 LEAST = 1e-30
-SHRINK = 2048.0
+SHRINK = 4096.0
 MESH = pl.DeviceIdType.MESH
 F32 = jnp.float32
 BF16 = jnp.bfloat16
@@ -19,32 +19,33 @@
 SLOTS = 5
 DN = 256
 DPART = 3
-NAMES = 'CSARDYXNQTFZB'
+DIRECT = 8
+NAMES = 'CSARDYXNQTFZBWME'
 PARTS = (
 (
-    ('C', 0, 0), ('C', 0, 1), ('C', 0, 2), ('Z', 0, 0), ('S', 0, 0), ('S', 0, 1), ('S', 1, 0), ('C', 0, 3),
-    ('S', 0, 2), ('S', 1, 1), ('C', 0, 4), ('S', 0, 3), ('S', 1, 2), ('A', 0, 0), ('C', 0, 5), ('A', 0, 1),
-    ('S', 0, 4), ('C', 0, 6), ('A', 0, 2), ('S', 0, 5), ('A', 1, 0), ('C', 0, 7), ('A', 0, 3), ('S', 0, 6),
-    ('A', 1, 1), ('R', 0, 0), ('A', 1, 2), ('C', 0, 8),
+    ('C', 0, 0), ('C', 0, 1), ('Z', 0, 0), ('S', 0, 0), ('S', 1, 0), ('C', 0, 2), ('W', 0, 0), ('S', 0, 1),
+    ('S', 1, 1), ('C', 0, 3), ('S', 0, 2), ('S', 1, 2), ('C', 0, 4), ('A', 0, 0), ('S', 0, 3), ('S', 1, 3),
+    ('C', 0, 5), ('A', 0, 1), ('S', 0, 4), ('A', 1, 0), ('S', 1, 4), ('C', 0, 6), ('A', 0, 2), ('S', 0, 5),
+    ('C', 0, 7), ('R', 0, 0), ('A', 0, 3), ('S', 0, 6), ('A', 1, 1), ('C', 0, 8),
 ),
 (
-    ('R', 0, 1), ('A', 0, 4), ('R', 0, 2), ('S', 0, 7), ('S', 1, 3), ('S', 1, 4), ('A', 0, 5), ('D', 0, 0),
-    ('R', 0, 3), ('S', 0, 8), ('R', 1, 0), ('D', 0, 1), ('A', 0, 6), ('R', 1, 1), ('R', 1, 2), ('S', 1, 5),
-    ('D', 0, 2), ('R', 0, 4), ('S', 1, 6), ('A', 0, 7), ('D', 0, 3), ('A', 1, 3), ('S', 1, 7), ('D', 0, 4),
-    ('R', 0, 5), ('A', 1, 4), ('D', 1, 0), ('A', 0, 8), ('R', 0, 6), ('S', 1, 8), ('D', 1, 1), ('A', 1, 5),
-    ('D', 0, 5), ('R', 0, 7), ('A', 1, 6), ('D', 0, 6), ('R', 1, 3), ('D', 1, 2), ('R', 1, 4), ('A', 1, 7),
-    ('R', 0, 8), ('D', 0, 7), ('A', 1, 8), ('D', 1, 3), ('Y', 0, 8), ('R', 1, 5), ('R', 1, 6), ('R', 1, 7),
-    ('D', 1, 4), ('R', 1, 8), ('D', 1, 5), ('D', 1, 6), ('D', 1, 7), ('Y', 1, 8),
+    ('R', 0, 1), ('S', 0, 7), ('A', 0, 4), ('A', 1, 2), ('A', 1, 3), ('R', 1, 0), ('S', 1, 5), ('A', 1, 4),
+    ('S', 0, 8), ('R', 0, 2), ('E', 0, 0), ('R', 0, 3), ('A', 0, 5), ('S', 1, 6), ('A', 0, 6), ('R', 1, 1),
+    ('S', 1, 7), ('D', 0, 3), ('R', 0, 4), ('A', 0, 7), ('S', 1, 8), ('R', 1, 2), ('E', 0, 1), ('R', 1, 3),
+    ('A', 1, 5), ('D', 0, 4), ('R', 1, 4), ('E', 0, 2), ('R', 0, 5), ('A', 0, 8), ('D', 1, 3), ('A', 1, 6),
+    ('R', 0, 6), ('D', 1, 4), ('A', 1, 7), ('D', 0, 5), ('R', 0, 7), ('D', 0, 6), ('R', 1, 5), ('A', 1, 8),
+    ('R', 0, 8), ('D', 0, 7), ('Y', 0, 8), ('R', 1, 6), ('R', 1, 7), ('D', 1, 5), ('R', 1, 8), ('D', 1, 6),
+    ('D', 1, 7), ('Y', 1, 8),
 ),
 (
-    ('X', 0, 0), ('Q', 0, 0), ('Q', 0, 1), ('Q', 0, 2), ('Q', 0, 3), ('Q', 0, 4), ('N', 0, 0), ('T', 0, 0),
-    ('T', 0, 1), ('X', 1, 0), ('T', 0, 2), ('T', 0, 3), ('Q', 0, 5), ('T', 0, 4), ('B', 0, 6), ('B', 0, 7),
-    ('T', 0, 5), ('F', 0, 0), ('B', 0, 8), ('T', 0, 6), ('F', 0, 1), ('N', 1, 0), ('T', 0, 7), ('T', 1, 6),
-    ('T', 1, 7), ('F', 0, 2), ('B', 0, 9), ('T', 0, 8), ('T', 1, 8), ('F', 0, 3), ('Q', 1, 0), ('F', 0, 4),
-    ('Q', 1, 1), ('T', 0, 9), ('T', 1, 9), ('F', 0, 5), ('F', 0, 6), ('Q', 1, 2), ('T', 1, 0), ('F', 0, 7),
-    ('T', 1, 1), ('Q', 1, 3), ('F', 1, 6), ('Q', 1, 4), ('T', 1, 2), ('F', 1, 7), ('F', 0, 8), ('Q', 1, 5),
-    ('T', 1, 3), ('F', 1, 8), ('T', 1, 4), ('F', 0, 9), ('T', 1, 5), ('F', 1, 9), ('F', 1, 0), ('F', 1, 1),
-    ('F', 1, 2), ('F', 1, 3), ('F', 1, 4), ('F', 1, 5),
+    ('X', 0, 0), ('Q', 0, 0), ('Q', 0, 1), ('N', 0, 0), ('Q', 0, 2), ('T', 0, 0), ('Q', 0, 3), ('T', 0, 1),
+    ('Q', 0, 4), ('M', 0, 0), ('X', 1, 0), ('T', 0, 2), ('T', 0, 3), ('B', 0, 5), ('T', 0, 4), ('B', 0, 6),
+    ('N', 1, 0), ('F', 0, 0), ('B', 0, 7), ('T', 0, 5), ('F', 0, 1), ('T', 1, 5), ('B', 0, 8), ('M', 1, 0),
+    ('T', 0, 6), ('T', 1, 6), ('T', 0, 7), ('F', 0, 2), ('T', 1, 7), ('B', 0, 9), ('T', 0, 8), ('F', 0, 3),
+    ('T', 1, 8), ('Q', 1, 0), ('F', 0, 4), ('Q', 1, 1), ('T', 0, 9), ('F', 0, 5), ('T', 1, 9), ('Q', 1, 2),
+    ('T', 1, 0), ('F', 1, 5), ('Q', 1, 3), ('F', 0, 6), ('T', 1, 1), ('Q', 1, 4), ('T', 1, 2), ('F', 1, 6),
+    ('F', 0, 7), ('T', 1, 3), ('F', 1, 7), ('T', 1, 4), ('F', 0, 8), ('F', 1, 8), ('F', 0, 9), ('F', 1, 9),
+    ('F', 1, 0), ('F', 1, 1), ('F', 1, 2), ('F', 1, 3), ('F', 1, 4),
 ),
 )
 
@@ -77,7 +78,7 @@
     sib = (z, y, chip * 2 + (1 - core))
     partner = (z, y, (1 - chip) * 2 + (1 - core))
     ypeer = (z, 1 - y, me)
-    hid_peers = [(z, y, (me + k) % 4) for k in (1, 2, 3)]
+    hid_peers = [sib, partner, (z, y, (1 - chip) * 2 + core)]
 
     def rcopy(src, dst, ss, rs, dev):
         return pltpu.make_async_remote_copy(src_ref=src, dst_ref=dst, send_sem=ss, recv_sem=rs,
@@ -104,7 +105,13 @@
         return pltpu.make_async_copy(wd_hbm.at[r, :], wd.at[r, :], wd_sem.at[p])
 
     def wq_copy(j):
-        return pltpu.make_async_copy(wq_hbm.at[:, span(j * CH, CH)], wq.at[j], wq_sem.at[j])
+        return pltpu.make_async_copy(wq_hbm.at[:, span(j * CH, CH)], wq.at[j], wq_sem.at[j // 2])
+
+    def wq_wait(j):
+        @pl.when(j % 2 == 0)
+        def _():
+            two = wq.at[pl.ds(j, 2)]
+            pltpu.make_async_copy(two, two, wq_sem.at[j // 2]).wait()
 
     def natural(g, h):
         return h * (rows // 2) + g * qr
@@ -150,29 +157,47 @@
         nb[r] = (x * (1.0 / u) * gain).astype(BF16)
 
     def stat_copy(t, k):
-        return rcopy(st_snd.at[t], st_rcv.at[t, k], sent.at[0], st_rs.at[t], hid_peers[k])
-
-    def stat_factors(t, which, r, n):
-        pltpu.make_async_copy(st_rcv.at[t], st_rcv.at[t], st_rs.at[t]).wait()
+        return rcopy(st_snd.at[t], st_rcv.at[t, k], sent.at[0], st_rs.at[t, min(k, 1)], hid_peers[k])
+
+    def factors(which, r, n, first, lanes):
+        packed = lanes[-1]
+        for k, v in enumerate(lanes[:-1]):
+            packed = jnp.where(lane_row == k, v, packed)
+        cols = packed.T
+        for k in range(len(lanes)):
+            fac[which, first + k, r] = jnp.broadcast_to(cols[:n, k:k + 1], (n, 128))
+
+    def larger(a, b):
+        return jnp.maximum(a[1:2], b[1:2]), jnp.maximum(a[2:3], b[2:3])
+
+    def pair_factors(t, which, r, n):
+        pltpu.make_async_copy(st_rcv.at[t, 0], st_rcv.at[t, 0], st_rs.at[t, 0]).wait()
+        u, v = larger(st_snd[t], st_rcv[t, 0])
+        factors(which, r, n, 0, [(m[1:2] / u) * (m[2:3] / v) for m in (st_snd[t], st_rcv[t, 0])])
+
+    def chip_factors(t, which, r, n):
+        pltpu.make_async_copy(st_rcv.at[t, 1:], st_rcv.at[t, 1:], st_rs.at[t, 1]).wait()
         total = (st_snd[t] + st_rcv[t, 0]) + (st_rcv[t, 1] + st_rcv[t, 2])
         scale = lax.rsqrt(total[0:1] / d_model + NORM_EPS)
-        rows_ = []
-        for msg in (st_snd[t], st_rcv[t, 2 * (1 - core)]):
-            v = msg[2:3]
-            rows_.append((scale * msg[1:2] * SHRINK) * jnp.minimum(v, 1.0))
-            rows_.append(jnp.maximum(v, 1.0))
-        packed = rows_[3]
-        for k in range(3):
-            packed = jnp.where(lane_row == k, rows_[k], packed)
-        cols = packed.T
-        for k in range(4):
-            fac[which, k, r] = jnp.broadcast_to(cols[:n, k:k + 1], (n, 128))
-
-    def pair_add(which, r, mine, theirs):
-        def scaled(v, k):
-            f = [jnp.concatenate([fac[which, 2 * k + i, r]] * (CH // 128), axis=1) for i in range(2)]
-            return v.astype(F32) * f[0] * f[1]
-        return (scaled(mine, 0) + scaled(theirs, 1)).astype(BF16)
+        lanes = []
+        for a, b in ((st_snd[t], st_rcv[t, 0]), (st_rcv[t, 1], st_rcv[t, 2])):
+            u, v = larger(a, b)
+            lanes += [(scale * u * SHRINK) * jnp.minimum(v, 1.0), jnp.maximum(v, 1.0)]
+        factors(which, r, n, 2, lanes)
+
+    def scaled_add(a, b, fa, fb, which, r):
+        def scaled(v, ks):
+            v = v.astype(F32)
+            for k in ks:
+                v = v * jnp.concatenate([fac[which, k, r]] * (v.shape[-1] // 128), axis=1)
+            return v
+        return (scaled(a, fa) + scaled(b, fb)).astype(BF16)
+
+    def pair_add(a, b, which, r):
+        return scaled_add(a, b, (0,), (1,), which, r)
+
+    def chip_add(a, b, which, r):
+        return scaled_add(a, b, (2, 3), (4, 5), which, r)
 
     pltpu.make_async_copy(xb, xb, in_sem.at[0]).wait()
     for c in gains:
@@ -228,20 +253,29 @@
         r = span(g * qr, qr)
         c = span(j * CH, CH)
         rr = held(g, own)
-        s_buf[:, r, c] = pair_add(0, rr, p_buf[:, rr, c], p_rcv[:, r, c])
+        s_buf[:, r, c] = pair_add(p_buf[:, rr, c], p_rcv[:, r, c], 0, rr)
         s_copy(g, j).start()
 
     def do_a(g, j):
         s_copy(g, j).wait_recv()
         r = span(g * qr, qr)
-        gu = add(s_buf[:, r, span(j * CH + chip * hc, hc)], s_rcv[:, r, span(j * hc, hc)]).astype(F32)
+        mine = s_buf[:, r, span(j * CH + chip * hc, hc)]
+        gu = chip_add(mine, s_rcv[:, r, span(j * hc, hc)], 0, held(g, own)).astype(F32)
         a_buf[g, span(own * qr, qr), span(j * CH + chip * hc, hc)] = (jax.nn.silu(gu[0]) * gu[1]).astype(BF16)
         ax_copy(g, j, chip).start()
+
+        @pl.when(j >= DIRECT)
+        def _():
+            piece = a_piece(g, j, own, chip)
+            rcopy(piece, piece, sent.at[4], ad_rs.at[g, j], hid_peers[2]).start()
         ad_copy(g, j, chip).start()
 
     def do_r(g, j):
         ax_copy(g, j, 1 - chip).wait_recv()
-        ad_copy(g, j, 1 - chip).start()
+
+        @pl.when(j < DIRECT)
+        def _():
+            ad_copy(g, j, 1 - chip).start()
 
     def down_operands(g, j):
         got = a_buf.at[g, span(other * qr, qr), span(j * CH, CH)]
@@ -256,6 +290,13 @@
         k = span(j * CH, CH)
         old = jnp.where(j == 0, 0.0, acc[g])
         acc[g] = old + dot(a_buf[g, :, k], wd[k, :])
+
+    def do_e(_, j):
+        for g in range(GROUPS):
+            down_operands(g, j)
+        k = span(j * CH, CH)
+        prod = dot(a_buf[:, :, k].reshape(rows, CH), wd[k, :]).reshape(GROUPS, gr, width)
+        acc[...] = jnp.where(j == 0, 0.0, acc[...]) + prod
 
     def dn_copy(g, n):
         return rcopy(dn_snd.at[g, n], dn_rcv.at[g, n], sent.at[5], dn_rs.at[g], ypeer)
@@ -284,10 +325,16 @@
             stat_copy(1 + g, k).start()
 
     def do_n(g, _):
-        stat_factors(1 + g, 1, span(g * gr, gr), gr)
+        pair_factors(1 + g, 1, span(g * gr, gr), gr)
+
+    def do_m(g, _):
+        chip_factors(1 + g, 1, span(g * gr, gr), gr)
 
     def do_z(_, __):
-        stat_factors(0, 0, pl.ds(0, rows), rows)
+        pair_factors(0, 0, pl.ds(0, rows), rows)
+
+    def do_w(_, __):
+        chip_factors(0, 0, pl.ds(0, rows), rows)
 
     def qp_ref(g, j, h):
         return wgu.at[0, 0, span(j * rows + g * gr + h * qr, qr)]
@@ -310,28 +357,28 @@
     def do_q(g, j):
         @pl.when(g == 0)
         def _():
-            wq_copy(j).wait()
+            wq_wait(j)
         wgu[0, 0, span(j * rows + g * gr, gr)] = dot(nb[span(g * gr, gr)], wq[j]).astype(BF16)
         qp_copy(g, j).start()
 
     def do_b(_, j):
-        wq_copy(j).wait()
+        wq_wait(j)
         wgu[0, 0, span(j * rows, rows)] = dot(nb[...], wq[j]).astype(BF16)
         for g in range(GROUPS):
             qp_copy(g, j).start()
 
     def do_t(g, j):
         qp_copy(g, j).wait_recv()
-        q_ref(2, g, j)[...] = pair_add(1, held(g, own), qp_ref(g, j, own)[...], q_ref(1, g, j)[...])
+        q_ref(2, g, j)[...] = pair_add(qp_ref(g, j, own)[...], q_ref(1, g, j)[...], 1, held(g, own))
         qs_copy(g, j).start()
 
     def do_f(g, j):
         qs_copy(g, j).wait_recv()
-        q_piece(g, j, own)[...] = add(q_ref(2, g, j)[...], q_ref(3, g, j)[...])
+        q_piece(g, j, own)[...] = chip_add(q_ref(2, g, j)[...], q_ref(3, g, j)[...], 1, held(g, own))
         qo_copy(g, j, own).start()
 
     tasks = dict(C=do_c, S=do_s, A=do_a, R=do_r, D=do_d, Y=do_y, X=do_x, N=do_n, Q=do_q, T=do_t, F=do_f,
-                 Z=do_z, B=do_b)
+                 Z=do_z, B=do_b, W=do_w, M=do_m, E=do_e)
 
     def run(kinds, kind, g, j):
         if len(kinds) == 1:
@@ -345,7 +392,7 @@
         codes = [NAMES.index(name) * 32 + g * 16 + j for name, g, j in part]
         codes += [len(NAMES) * 32] * (-len(codes) % 3)
         kinds = sorted({c // 32 for c in codes})
-        words = [codes[i] + codes[i + 1] * 512 + codes[i + 2] * 512 * 512 for i in range(0, len(codes), 3)]
+        words = [codes[i] + codes[i + 1] * 1024 + codes[i + 2] * 1024 * 1024 for i in range(0, len(codes), 3)]
 
         @pl.loop(0, len(words))
         def _(i):
@@ -354,10 +401,10 @@
                 word = jnp.where(i == n, jnp.int32(w), word)
 
             def step(_, word):
-                code = lax.rem(word, jnp.int32(512))
+                code = lax.rem(word, jnp.int32(1024))
                 gj = lax.rem(code, jnp.int32(32))
                 run(kinds, lax.div(code, jnp.int32(32)), lax.div(gj, jnp.int32(16)), lax.rem(gj, jnp.int32(16)))
-                return lax.div(word, jnp.int32(512))
+                return lax.div(word, jnp.int32(1024))
             lax.fori_loop(0, 3, step, word)
 
     for g in range(GROUPS):
@@ -367,6 +414,14 @@
     for i, ref in enumerate((st_rcv, p_rcv, s_rcv, a_buf.at[:, :qr, :n_g * hc], a_half, dn_rcv,
                              q_part, q_part, q_out.at[:rows // 2])):
         pltpu.make_async_copy(ref, ref, sent.at[i]).wait()
+
+
+def write_out(x2, q, x2_hbm, q_hbm, sem):
+    cps = [pltpu.make_async_copy(x2, x2_hbm, sem.at[0]), pltpu.make_async_copy(q, q_hbm, sem.at[1])]
+    for c in cps:
+        c.start()
+    for c in cps:
+        c.wait()
 
 
 def solution(mesh):
@@ -381,7 +436,7 @@
         n_g, n_q, n_d = ff // CH, qn // CH, width // DN
         dma = pltpu.SemaphoreType.DMA
         gg, gq = dma((GROUPS, n_g)), dma((GROUPS, n_q))
-        return pl.pallas_call(
+        x2, q = pl.pallas_call(
             functools.partial(kernel, width * hid_ways),
             out_shape=(pltpu.VMEM((rows, width), BF16), pltpu.VMEM((rows, qn), BF16)),
             in_specs=[pl.BlockSpec(memory_space=pltpu.HBM)] * 7,
@@ -391,7 +446,7 @@
                 pltpu.VMEM((width,), F32),
                 pltpu.VMEM((width,), F32),
                 pltpu.VMEM((rows, width), BF16),
-                pltpu.VMEM((2, 4, rows, 128), F32),
+                pltpu.VMEM((2, 6, rows, 128), F32),
                 pltpu.VMEM((SLOTS, 2, width, CH), BF16),
                 pltpu.VMEM((ff, width), BF16),
                 pltpu.VMEM((n_q, width, CH), BF16),
@@ -405,12 +460,20 @@
                 pltpu.VMEM((GROUPS, n_d, gr, DN), BF16),
                 pltpu.VMEM((1 + GROUPS, 8, 128), F32),
                 pltpu.VMEM((1 + GROUPS, 3, 8, 128), F32),
-                dma((3,)), dma((SLOTS,)), dma((n_g // DPART,)), dma((n_q,)), dma((9,)),
-                gq, gq, gq, gg, dma((GROUPS,)), dma((1 + GROUPS,)),
+                dma((3,)), dma((SLOTS,)), dma((n_g // DPART,)), dma((n_q // 2,)), dma((9,)),
+                gq, gq, gq, gg, dma((GROUPS,)), dma((1 + GROUPS, 2)),
             ],
             compiler_params=pltpu.CompilerParams(
                 collective_id=0, has_side_effects=True, vmem_limit_bytes=65400000),
         )(residual, gain_mlp, gain_attn, w_gate, w_up, w_down, w_qkv)
+        return pl.pallas_call(
+            write_out,
+            out_shape=(jax.ShapeDtypeStruct((rows, width), BF16), jax.ShapeDtypeStruct((rows, qn), BF16)),
+            in_specs=[pl.BlockSpec(memory_space=pltpu.VMEM)] * 2,
+            out_specs=(pl.BlockSpec(memory_space=pltpu.HBM),) * 2,
+            scratch_shapes=[dma((2,))],
+            compiler_params=pltpu.CompilerParams(vmem_limit_bytes=1 << 20),
+        )(x2, q)
 
     return jax.shard_map(
         device_step, mesh=mesh,

time: 48.7 us -> 47.4 us (0.973)
  local copies, waits for them, and re-layouts: 1.61 us -> 0 us
    unnamed x2 -> x0, local copies, waits for them, and re-layouts: 1.61 us -> none
    pallas_call x0 -> x1, Pallas kernels: none -> 1.02 us  [device_step(): pl.pallas_call(write_out, out_shape=(jax.ShapeDtypeStruct((rows, width),...]
    pallas_call x1, Pallas kernels: 46.4 us -> 45.6 us  [device_step(): pl.pallas_call(functools.partial(kernel, width * hid_ways), out_shape=(pl...]
where the time goes in v5:
time: 47.4 us; the launch traced here: 47.3 us
  Pallas kernels  46.6 us (98%)
  between operations  0.64 us (1%)
    pallas_call x1, Pallas kernels, device_step(): pl.pallas_call(functools.partial(kernel, width * hid_ways), out_shape=(pl...  45.6 us
    pallas_call x1, Pallas kernels, device_step(): pl.pallas_call(write_out, out_shape=(jax.ShapeDtypeStruct((rows, width),...  1.02 us

profile of v5, /device:TPU:0, one launch (start us, length us, event | category | flops | bytes accessed | tf_op | source)
XLA Modules:
  0.0 47.3 jit_solution(4235626781015291245)
XLA Ops:
  0.6 45.6 %shard_map.86 = (bf16[64,1280]{1,0:T(8,128)(2,1)S(1)}, bf16[64,7680]{1,0:T(8,128)(2,1)S(1)}) custom-call(bf16[64,1280]{1,0:T(8,128)(2,1)} %x_hbm.1, f32[1280]{0:T(1024)} %g1_hbm.1, f32[1280]{0:T(1024)} %g2_hbm.1, bf16[1280,6912]{1,0:T(8,128)(2,1)} %wg_hbm.1, bf16[1280,6912]{1,0:T(8,128)(2,1)} %wu_hbm.1, bf16[6912,1280]{1,0:T(8,128)(2,1)} %wd_hbm.1, ...), custom_call_target="tpu_custom_call" | custom-call | tf_op jit(solution)/shard_map/pallas_call | solution.py:439
  46.2 1.0 %shard_map.87 = (bf16[64,1280]{1,0:T(8,128)(2,1)}, bf16[64,7680]{1,0:T(8,128)(2,1)}) custom-call(bf16[64,1280]{1,0:T(8,128)(2,1)S(1)} %get-tuple-element.4.x2, bf16[64,7680]{1,0:T(8,128)(2,1)S(1)} %get-tuple-element.5.q), custom_call_target="tpu_custom_call" | custom-call | tf_op jit(solution)/shard_map/pallas_call | solution.py:469

commit v6 on v5

--- a/solution.py
+++ b/solution.py
@@ -22,31 +22,18 @@
 DIRECT = 8
 NAMES = 'CSARDYXNQTFZBWME'
 PARTS = (
-(
-    ('C', 0, 0), ('C', 0, 1), ('Z', 0, 0), ('S', 0, 0), ('S', 1, 0), ('C', 0, 2), ('W', 0, 0), ('S', 0, 1),
-    ('S', 1, 1), ('C', 0, 3), ('S', 0, 2), ('S', 1, 2), ('C', 0, 4), ('A', 0, 0), ('S', 0, 3), ('S', 1, 3),
-    ('C', 0, 5), ('A', 0, 1), ('S', 0, 4), ('A', 1, 0), ('S', 1, 4), ('C', 0, 6), ('A', 0, 2), ('S', 0, 5),
-    ('C', 0, 7), ('R', 0, 0), ('A', 0, 3), ('S', 0, 6), ('A', 1, 1), ('C', 0, 8),
-),
-(
-    ('R', 0, 1), ('S', 0, 7), ('A', 0, 4), ('A', 1, 2), ('A', 1, 3), ('R', 1, 0), ('S', 1, 5), ('A', 1, 4),
-    ('S', 0, 8), ('R', 0, 2), ('E', 0, 0), ('R', 0, 3), ('A', 0, 5), ('S', 1, 6), ('A', 0, 6), ('R', 1, 1),
-    ('S', 1, 7), ('D', 0, 3), ('R', 0, 4), ('A', 0, 7), ('S', 1, 8), ('R', 1, 2), ('E', 0, 1), ('R', 1, 3),
-    ('A', 1, 5), ('D', 0, 4), ('R', 1, 4), ('E', 0, 2), ('R', 0, 5), ('A', 0, 8), ('D', 1, 3), ('A', 1, 6),
-    ('R', 0, 6), ('D', 1, 4), ('A', 1, 7), ('D', 0, 5), ('R', 0, 7), ('D', 0, 6), ('R', 1, 5), ('A', 1, 8),
-    ('R', 0, 8), ('D', 0, 7), ('Y', 0, 8), ('R', 1, 6), ('R', 1, 7), ('D', 1, 5), ('R', 1, 8), ('D', 1, 6),
-    ('D', 1, 7), ('Y', 1, 8),
-),
-(
-    ('X', 0, 0), ('Q', 0, 0), ('Q', 0, 1), ('N', 0, 0), ('Q', 0, 2), ('T', 0, 0), ('Q', 0, 3), ('T', 0, 1),
-    ('Q', 0, 4), ('M', 0, 0), ('X', 1, 0), ('T', 0, 2), ('T', 0, 3), ('B', 0, 5), ('T', 0, 4), ('B', 0, 6),
-    ('N', 1, 0), ('F', 0, 0), ('B', 0, 7), ('T', 0, 5), ('F', 0, 1), ('T', 1, 5), ('B', 0, 8), ('M', 1, 0),
-    ('T', 0, 6), ('T', 1, 6), ('T', 0, 7), ('F', 0, 2), ('T', 1, 7), ('B', 0, 9), ('T', 0, 8), ('F', 0, 3),
-    ('T', 1, 8), ('Q', 1, 0), ('F', 0, 4), ('Q', 1, 1), ('T', 0, 9), ('F', 0, 5), ('T', 1, 9), ('Q', 1, 2),
-    ('T', 1, 0), ('F', 1, 5), ('Q', 1, 3), ('F', 0, 6), ('T', 1, 1), ('Q', 1, 4), ('T', 1, 2), ('F', 1, 6),
-    ('F', 0, 7), ('T', 1, 3), ('F', 1, 7), ('T', 1, 4), ('F', 0, 8), ('F', 1, 8), ('F', 0, 9), ('F', 1, 9),
-    ('F', 1, 0), ('F', 1, 1), ('F', 1, 2), ('F', 1, 3), ('F', 1, 4),
-),
+    (
+        'C0C1Z0S0s0C2W0S1s1C3S2s2C4A0S3s3C5A1S4a0s4C6A2S5C7R0A3S6a1C8',
+    ),
+    (
+        'R1S7A4a2a3r0s5a4S8R2E0R3A5s6A6r1s7D3R4A7s8r2E1r3a5D4r4E2R5A8',
+        'd3a6R6d4a7D5R7D6r5a8R8D7Y8r6r7d5r8d6d7y8',
+    ),
+    (
+        'X0Q0Q1N0Q2T0Q3T1Q4M0x0T2T3B5T4B6n0F0B7T5F1t5B8m0T6t6T7F2t7B9',
+        'T8F3t8q0F4q1T9F5t9q2t0f5q3F6t1q4t2f6F7t3f7t4F8f8F9f9f0f1f2f3',
+        'f4',
+    ),
 )
 
 
@@ -232,9 +219,8 @@
         c = span(j * CH, CH)
         gu_wait(j)
 
-        def one(i):
+        for i in range(2):
             p_buf[i, :, c] = dot(nb[...], wgu[j % SLOTS, i]).astype(BF16)
-        each(2, one)
         for g in range(GROUPS):
             p_copy(g, j).start()
 
@@ -389,7 +375,8 @@
         lax.cond(kind < high[0], lambda: run(low, kind, g, j), lambda: run(high, kind, g, j))
 
     for part in PARTS:
-        codes = [NAMES.index(name) * 32 + g * 16 + j for name, g, j in part]
+        text = ''.join(part)
+        codes = [NAMES.index(c.upper()) * 32 + c.islower() * 16 + int(d) for c, d in zip(text[::2], text[1::2])]
         codes += [len(NAMES) * 32] * (-len(codes) % 3)
         kinds = sorted({c // 32 for c in codes})
         words = [codes[i] + codes[i + 1] * 1024 + codes[i + 2] * 1024 * 1024 for i in range(0, len(codes), 3)]

time: 47.4 us -> 46.5 us (0.981)
  Pallas kernels: 46.6 us -> 45.8 us
    pallas_call x1, Pallas kernels: 45.6 us -> 44.8 us  [device_step(): pl.pallas_call(functools.partial(kernel, width * hid_ways), out_shape=(pl...]
where the time goes in v6:
time: 46.5 us; the launch traced here: 46.4 us
  Pallas kernels  45.8 us (98%)
  between operations  0.64 us (1%)
    pallas_call x1, Pallas kernels, device_step(): pl.pallas_call(functools.partial(kernel, width * hid_ways), out_shape=(pl...  44.8 us
    pallas_call x1, Pallas kernels, device_step(): pl.pallas_call(write_out, out_shape=(jax.ShapeDtypeStruct((rows, width),...  1.02 us

profile of v6, /device:TPU:0, one launch (start us, length us, event | category | flops | bytes accessed | tf_op | source)
XLA Modules:
  0.0 46.4 jit_solution(13985702304976137986)
XLA Ops:
  0.6 44.8 %shard_map.86 = (bf16[64,1280]{1,0:T(8,128)(2,1)S(1)}, bf16[64,7680]{1,0:T(8,128)(2,1)S(1)}) custom-call(bf16[64,1280]{1,0:T(8,128)(2,1)} %x_hbm.1, f32[1280]{0:T(1024)} %g1_hbm.1, f32[1280]{0:T(1024)} %g2_hbm.1, bf16[1280,6912]{1,0:T(8,128)(2,1)} %wg_hbm.1, bf16[1280,6912]{1,0:T(8,128)(2,1)} %wu_hbm.1, bf16[6912,1280]{1,0:T(8,128)(2,1)} %wd_hbm.1, ...), custom_call_target="tpu_custom_call" | custom-call | tf_op jit(solution)/shard_map/pallas_call | solution.py:426
  45.4 1.0 %shard_map.87 = (bf16[64,1280]{1,0:T(8,128)(2,1)}, bf16[64,7680]{1,0:T(8,128)(2,1)}) custom-call(bf16[64,1280]{1,0:T(8,128)(2,1)S(1)} %get-tuple-element.4.x2, bf16[64,7680]{1,0:T(8,128)(2,1)S(1)} %get-tuple-element.5.q), custom_call_target="tpu_custom_call" | custom-call | tf_op jit(solution)/shard_map/pallas_call | solution.py:456

commit v7 on v6

--- a/solution.py
+++ b/solution.py
@@ -23,15 +23,15 @@
 NAMES = 'CSARDYXNQTFZBWME'
 PARTS = (
     (
-        'C0C1Z0S0s0C2W0S1s1C3S2s2C4A0S3s3C5A1S4a0s4C6A2S5C7R0A3S6a1C8',
+        'C0C1Z0S0s0C2W0S1s1C3S2s2C4A0S3s3C5A1S4a0s4C6A2S5C7A3S6a1C8',
     ),
     (
-        'R1S7A4a2a3r0s5a4S8R2E0R3A5s6A6r1s7D3R4A7s8r2E1r3a5D4r4E2R5A8',
-        'd3a6R6d4a7D5R7D6r5a8R8D7Y8r6r7d5r8d6d7y8',
+        'S7R1A4a2a3s5R0r0R2E0a4R3A5S8s6A6r1s7D3R4r2A7s8E1r3a5D4r4E2R5',
+        'A8d3a6R6d4D5R7D6a7r5a8R8D7Y8r6d5r8r7d6d7y8',
     ),
     (
-        'X0Q0Q1N0Q2T0Q3T1Q4M0x0T2T3B5T4B6n0F0B7T5F1t5B8m0T6t6T7F2t7B9',
-        'T8F3t8q0F4q1T9F5t9q2t0f5q3F6t1q4t2f6F7t3f7t4F8f8F9f9f0f1f2f3',
+        'X0Q0Q1Q2N0T0Q3T1Q4M0x0T2T3B5T4B6n0F0B7T5F1t5B8m0T6t6T7F2t7B9',
+        'T8q3F3t8q0F4q1T9F5q2t0t9q4t2F6t1f5f6F7t3F8f7t4f8F9f9f0f1f2f3',
         'f4',
     ),
 )

time: 46.5 us -> 46.2 us (level)
  no operation moved by 1% of the time
where the time goes in v7:
time: 46.2 us; the launch traced here: 46.1 us
  Pallas kernels  45.4 us (98%)
  between operations  0.64 us (1%)
    pallas_call x1, Pallas kernels, device_step(): pl.pallas_call(functools.partial(kernel, width * hid_ways), out_shape=(pl...  44.4 us
    pallas_call x1, Pallas kernels, device_step(): pl.pallas_call(write_out, out_shape=(jax.ShapeDtypeStruct((rows, width),...  1.02 us

profile of v7, /device:TPU:0, one launch (start us, length us, event | category | flops | bytes accessed | tf_op | source)
XLA Modules:
  0.0 46.1 jit_solution(15786214642872753027)
XLA Ops:
  0.6 44.4 %shard_map.86 = (bf16[64,1280]{1,0:T(8,128)(2,1)S(1)}, bf16[64,7680]{1,0:T(8,128)(2,1)S(1)}) custom-call(bf16[64,1280]{1,0:T(8,128)(2,1)} %x_hbm.1, f32[1280]{0:T(1024)} %g1_hbm.1, f32[1280]{0:T(1024)} %g2_hbm.1, bf16[1280,6912]{1,0:T(8,128)(2,1)} %wg_hbm.1, bf16[1280,6912]{1,0:T(8,128)(2,1)} %wu_hbm.1, bf16[6912,1280]{1,0:T(8,128)(2,1)} %wd_hbm.1, ...), custom_call_target="tpu_custom_call" | custom-call | tf_op jit(solution)/shard_map/pallas_call | solution.py:426
  45.1 1.0 %shard_map.87 = (bf16[64,1280]{1,0:T(8,128)(2,1)}, bf16[64,7680]{1,0:T(8,128)(2,1)}) custom-call(bf16[64,1280]{1,0:T(8,128)(2,1)S(1)} %get-tuple-element.4.x2, bf16[64,7680]{1,0:T(8,128)(2,1)S(1)} %get-tuple-element.5.q), custom_call_target="tpu_custom_call" | custom-call | tf_op jit(solution)/shard_map/pallas_call | solution.py:456
